TPU v7x, 32 devices: a whole 2x2x4 slice. The times are simulated.
32 devices in a mesh: layer: 8 (over z, x), split: 4 (over y, core).
Axes of the slice: x: 2, y: 2, z: 4, core: 2. Of those that a mesh axis runs over, the one named last changes fastest.
Arguments:
- right_side: float32 [32, 512, 128], P('layer', 'split'), may hold values from -6 to 6
- diagonal: float32 [32, 512, 128], P('layer', 'split'), may hold values from 0.1 to 1
- inverses: float32 [32, 512, 512], P('layer', None, 'split'), may hold values from -1 to 1, as said below
Outputs:
- solution_field: float32 [32, 512, 128], P('layer', 'split')
- residual: float32 [32, 512, 128], P('layer', 'split')
Inputs may be any that keep to these rules, and one draw needn't show every extreme that they name: `inverses`: each plane's inverse is a diagonal matrix with entries between 0.5 and 1 plus a dense coupling with zero diagonal and spectral norm below 0.2.
All inputs are finite; a program needn't handle non-finite values.
Results may differ from a plain program's by a relative error of at most 0.0003.
Values sent between devices are 32-bit elements; how exact they have to be, the bound alone decides.
No kernel may reach another device: no remote copies, remote signals or barrier semaphores. Data moves between devices by JAX's collectives and lax.ppermute only.
A program may use at most 64 MiB of HBM per device.

v0:
```python
import jax
import jax.numpy as jnp
from jax import lax
from jax.sharding import PartitionSpec as P


def with_halo(x, sides, width):
    for axis, dim in sides:
        size, length = (lax.axis_size(axis), x.shape[dim])
        up = [(i, (i + 1) % size) for i in range(size - 1)]
        down = [(j, i) for i, j in up]
        last = lax.slice_in_dim(x, length - width, length, axis=dim)
        first = lax.slice_in_dim(x, 0, width, axis=dim)
        before = lax.ppermute(last, axis, up)
        after = lax.ppermute(first, axis, down)
        x = jnp.concatenate([before, x, after], axis=dim)
    return x


def from_behind(block, axis, distance):
    devices = range(lax.axis_size(axis))
    route = [(i - distance, i) for i in devices if i - distance in devices]
    return lax.ppermute(block, axis, route)


def stencil(values, diagonal):
    padded = with_halo(values, (("layer", 0), ("split", 1)), 1)
    beside = padded[2:, 1:-1, :] + padded[:-2, 1:-1, :]
    beside = beside + padded[1:-1, 2:, :] + padded[1:-1, :-2, :]
    centre_part = padded[1:-1, 1:-1, :]
    y_upper = jnp.pad(centre_part[:, :, 1:], ((0, 0), (0, 0), (0, 1)))
    y_lower = jnp.pad(centre_part[:, :, :-1], ((0, 0), (0, 0), (1, 0)))
    return (6.0 + diagonal) * values - beside - y_upper - y_lower


def down_local(matrices, portion, carried):

    def down_advance(state, inputs):
        matrix, source = inputs
        state = jnp.dot(matrix, source + state, precision=lax.Precision.HIGHEST)
        return (state, state)

    return lax.scan(down_advance, carried, (matrices, portion))


def up_local(matrices, portion, carried):

    def up_advance(state, inputs):
        matrix, below = inputs
        state = below + jnp.dot(matrix, state, precision=lax.Precision.HIGHEST)
        return (state, state)

    return lax.scan(up_advance, carried, (matrices, portion), reverse=True)


def chain_sweep(sweep_fn, matrices, source, sender, anchor, nblocks):
    depth_count = lax.axis_size("layer")
    block_width = source.shape[2] // nblocks
    plane_shape = (source.shape[1], block_width)
    result = jnp.zeros_like(source)
    incoming = jnp.zeros(plane_shape, jnp.float32)

    def chain_advance(turn, state):
        result, incoming = state
        block_raw = turn - anchor
        active = jnp.logical_and(block_raw >= 0, block_raw < nblocks)

        def working(unused):
            return sweep_fn(matrices, source, incoming)

        def resting(unused):
            return (jnp.zeros(plane_shape, jnp.float32), jnp.zeros_like(source))

        outgoing, stacked = lax.cond(active, working, resting, None)
        previous = result
        result = jnp.where(active, stacked, previous)
        return (result, sender(outgoing))

    result, incoming = lax.fori_loop(
        0, depth_count + nblocks - 1, chain_advance, (result, incoming)
    )
    return result


def per_device(right_side, diagonal, inverses):
    matrices = lax.all_gather(inverses, "split", axis=2, tiled=True)
    columns = lax.all_to_all(right_side, "split", split_axis=2, concat_axis=1, tiled=True)
    nblocks = 1
    own_index = lax.axis_index("layer")
    depth_count = lax.axis_size("layer")
    applied_rhs = stencil(right_side, diagonal)

    def send_down(values):
        return from_behind(values, "layer", 1)

    def send_up(values):
        return from_behind(values, "layer", -1)

    lower_sweep = chain_sweep(down_local, matrices, columns, send_down, own_index, nblocks)
    upper_sweep = chain_sweep(
        up_local, matrices, lower_sweep, send_up, depth_count - 1 - own_index, nblocks
    )
    direction = lax.all_to_all(upper_sweep, "split", split_axis=1, concat_axis=2, tiled=True)
    image = stencil(direction, diagonal)
    applied_image = stencil(image, diagonal)
    sums_all = lax.psum(
        (
            jnp.sum(right_side * right_side),
            jnp.sum(right_side * image),
            jnp.sum(applied_rhs * right_side),
            jnp.sum(applied_rhs * image),
            jnp.sum(applied_image * right_side),
            jnp.sum(applied_image * image),
            jnp.sum(applied_rhs * applied_rhs),
            jnp.sum(applied_rhs * applied_image),
            jnp.sum(applied_image * applied_image),
        ),
        ("layer", "split"),
    )
    (
        norm_sq,
        curv_sum,
        rhs_rhs,
        rhs_image,
        image_rhs,
        image_image,
        arhs_arhs,
        arhs_aimage,
        aimage_aimage,
    ) = sums_all
    step_alpha = norm_sq / curv_sum
    middle = right_side - step_alpha * image
    tangent = applied_rhs - step_alpha * applied_image
    cross_sum = (
        rhs_rhs - step_alpha * (rhs_image + image_rhs) + step_alpha * step_alpha * image_image
    )
    self_sum = arhs_arhs - 2.0 * step_alpha * arhs_aimage + step_alpha * step_alpha * aimage_aimage
    step_omega = cross_sum / self_sum
    solution_field = step_alpha * direction + step_omega * middle
    residual = middle - step_omega * tangent
    return (solution_field, residual)


def solution(mesh):
    placed = (P("layer", "split", None), P("layer", "split", None), P("layer", None, "split"))
    return jax.shard_map(
        per_device,
        mesh=mesh,
        in_specs=placed,
        out_specs=(P("layer", "split", None), P("layer", "split", None)),
        check_vma=False,
    )
```

profile of v0, /device:TPU:0, one launch (start us, length us, event | category | flops | bytes accessed | tf_op | source)
XLA Modules:
  0.0 438.2 jit_solution(2182941142321325081)
XLA Ops:
  7.9 1.8 copy.44
  9.7 4.3 all-to-all-start
  16.4 4.7 %collective-permute-start.7 = (f32[1,128,128]{1,2,0:T(8,128)S(1)}, f32[1,128,128]{1,2,0:T(8,128)S(1)}, u32[]{:S(2)}, u32[]{:S(2)}) collective-permute-start(f32[1,128,128]{1,2,0:T(8,128)S(1)} %get-tuple-element.506), channel_id=1, source_target_pairs={{0,4},{4,8},{8,12},{12,16},{16,20},{20,24},{24,28},{1,5},{5,9},{9,... | collective-permute-start | bytes 196616 | tf_op jit(solution)/shard_map/ppermute | solution.py:14
  23.9 23.4 %all-gather.2.cloned.1.call-done = f32[4,512,512]{2,1,0:T(8,128)} async-done(((f32[4,512,128]{2,1,0:T(8,128)}), f32[4,512,512]{2,1,0:T(8,128)}) %all-gather.2.cloned.1.call-update) | async-done | bytes 4194320 | tf_op jit(solution)/shard_map/all_gather | solution.py:86
  47.3 102.0 %while.60 = (s32[]{:T(128)}, f32[4,512,32]{1,2,0:T(8,128)S(1)}, f32[512,32]{0,1:T(8,128)S(1)}, s32[]{:T(128)}, f32[4,512,512]{2,1,0:T(8,128)}, /*index=5*/f32[4,512,32]{1,2,0:T(8,128)S(1)}, s32[]{:T(128)}, s32[]{:T(128)}) while((s32[]{:T(128)}, f32[4,512,32]{1,2,0:T(8,128)S(1)}, f32[512,32]{0,1:T(8,128)S(1)}, s32[]{:T(128)}, ...), condition=%wide.region_7.8_spmd.clone, body=%wide.region_2.7_spmd.clone.sunk | while | flops 100810760 | bytes 2623315 | solution.py:79
  47.3 11.7 %conditional.6 = (f32[512,32]{0,1:T(8,128)S(1)}, f32[4,512,32]{1,2,0:T(8,128)}) conditional(s32[]{:T(128)} %convert_element_type.26, () %tuple.150, (f32[4,512,512]{2,1,0:T(8,128)}, f32[4,512,32]{1,2,0:T(8,128)S(1)}, f32[512,32]{0,1:T(8,128)S(1)}) %tuple.151), branch_computations={%region_3.3_spmd, %region_4.6_spmd} | conditional | flops 100679680 | bytes 1574541 | solution.py:74
  47.3 11.7 %while.58 = (s32[]{:T(128)}, f32[512,32]{0,1:T(8,128)S(1)}, f32[4,512,32]{1,2,0:T(8,128)}, f32[4,512,512]{2,1,0:T(8,128)}, f32[4,512,32]{1,2,0:T(8,128)S(1)}, /*index=5*/s32[]{:T(128)}) while((s32[]{:T(128)}, f32[512,32]{0,1:T(8,128)S(1)}, f32[4,512,32]{1,2,0:T(8,128)}, f32[4,512,512]{2,1,0:T(8,128)}, f32[4,512,32]{1,2,0:T(8,128)S(1)}, ...), condition=%wide.region_6.5_spmd, body=%wide.region_5.4_spmd.sunk | while | flops 100679680 | bytes 1443397 | solution.py:43
  47.3 2.9 bitcast_dynamic-update-slice_fusion.5
  50.2 2.9 bitcast_dynamic-update-slice_fusion.5
  53.1 2.9 bitcast_dynamic-update-slice_fusion.5
  56.1 2.9 bitcast_dynamic-update-slice_fusion.5
  63.1 15.4 %collective-permute-start.1 = (f32[512,32]{0,1:T(8,128)S(1)}, f32[512,32]{0,1:T(8,128)S(1)}, u32[]{:S(2)}, u32[]{:S(2)}) collective-permute-start(f32[512,32]{0,1:T(8,128)S(1)} %get-tuple-element.643), channel_id=1, source_target_pairs={{0,4},{4,8},{8,12},{12,16},{16,20},{20,24},{24,28},{1,5},{5,9},{9,... | collective-permute-start | bytes 196616 | tf_op jit(solution)/shard_map/while/body/eval_jaxpr/ppermute | solution.py:23
  78.5 1.8 collective-permute-done.1
  81.1 4.3 collective-permute-start.1
  85.4 1.8 collective-permute-done.1
  87.9 13.8 %collective-permute-start.1 = (f32[512,32]{0,1:T(8,128)S(1)}, f32[512,32]{0,1:T(8,128)S(1)}, u32[]{:S(2)}, u32[]{:S(2)}) collective-permute-start(f32[512,32]{0,1:T(8,128)S(1)} %get-tuple-element.643), channel_id=1, source_target_pairs={{0,4},{4,8},{8,12},{12,16},{16,20},{20,24},{24,28},{1,5},{5,9},{9,... | collective-permute-start | bytes 196616 | tf_op jit(solution)/shard_map/while/body/eval_jaxpr/ppermute | solution.py:23
  101.9 1.8 collective-permute-done.1
  104.4 5.2 %collective-permute-start.1 = (f32[512,32]{0,1:T(8,128)S(1)}, f32[512,32]{0,1:T(8,128)S(1)}, u32[]{:S(2)}, u32[]{:S(2)}) collective-permute-start(f32[512,32]{0,1:T(8,128)S(1)} %get-tuple-element.643), channel_id=1, source_target_pairs={{0,4},{4,8},{8,12},{12,16},{16,20},{20,24},{24,28},{1,5},{5,9},{9,... | collective-permute-start | bytes 196616 | tf_op jit(solution)/shard_map/while/body/eval_jaxpr/ppermute | solution.py:23
  109.6 1.8 collective-permute-done.1
  112.1 12.0 %collective-permute-start.1 = (f32[512,32]{0,1:T(8,128)S(1)}, f32[512,32]{0,1:T(8,128)S(1)}, u32[]{:S(2)}, u32[]{:S(2)}) collective-permute-start(f32[512,32]{0,1:T(8,128)S(1)} %get-tuple-element.643), channel_id=1, source_target_pairs={{0,4},{4,8},{8,12},{12,16},{16,20},{20,24},{24,28},{1,5},{5,9},{9,... | collective-permute-start | bytes 196616 | tf_op jit(solution)/shard_map/while/body/eval_jaxpr/ppermute | solution.py:23
  124.3 1.8 collective-permute-done.1
  126.8 5.2 %collective-permute-start.1 = (f32[512,32]{0,1:T(8,128)S(1)}, f32[512,32]{0,1:T(8,128)S(1)}, u32[]{:S(2)}, u32[]{:S(2)}) collective-permute-start(f32[512,32]{0,1:T(8,128)S(1)} %get-tuple-element.643), channel_id=1, source_target_pairs={{0,4},{4,8},{8,12},{12,16},{16,20},{20,24},{24,28},{1,5},{5,9},{9,... | collective-permute-start | bytes 196616 | tf_op jit(solution)/shard_map/while/body/eval_jaxpr/ppermute | solution.py:23
  132.0 1.8 collective-permute-done.1
  134.6 12.9 %collective-permute-start.1 = (f32[512,32]{0,1:T(8,128)S(1)}, f32[512,32]{0,1:T(8,128)S(1)}, u32[]{:S(2)}, u32[]{:S(2)}) collective-permute-start(f32[512,32]{0,1:T(8,128)S(1)} %get-tuple-element.643), channel_id=1, source_target_pairs={{0,4},{4,8},{8,12},{12,16},{16,20},{20,24},{24,28},{1,5},{5,9},{9,... | collective-permute-start | bytes 196616 | tf_op jit(solution)/shard_map/while/body/eval_jaxpr/ppermute | solution.py:23
  147.6 1.8 collective-permute-done.1
  149.3 177.3 %while.61 = (s32[]{:T(128)}, f32[4,512,32]{1,2,0:T(8,128)S(1)}, f32[512,32]{0,1:T(8,128)S(1)}, s32[]{:T(128)}, f32[4,512,32]{1,2,0:T(8,128)S(1)}, /*index=5*/f32[4,512,512]{2,1,0:T(8,128)}, s32[]{:T(128)}, s32[]{:T(128)}) while((s32[]{:T(128)}, f32[4,512,32]{1,2,0:T(8,128)S(1)}, f32[512,32]{0,1:T(8,128)S(1)}, s32[]{:T(128)}, ...), condition=%wide.region_13.14_spmd.clone, body=%wide.region_8.13_spmd.clone.sunk | while | flops 100810760 | bytes 2884979 | solution.py:79
  151.5 6.0 %collective-permute-done = f32[512,32]{0,1:T(8,128)S(1)} collective-permute-done((f32[512,32]{0,1:T(8,128)S(1)}, f32[512,32]{0,1:T(8,128)S(1)}, u32[]{:S(2)}, u32[]{:S(2)}) %collective-permute-start) | collective-permute-done | bytes 65568 | tf_op jit(solution)/shard_map/while/body/eval_jaxpr/ppermute | solution.py:23
  159.6 13.5 %collective-permute-done = f32[512,32]{0,1:T(8,128)S(1)} collective-permute-done((f32[512,32]{0,1:T(8,128)S(1)}, f32[512,32]{0,1:T(8,128)S(1)}, u32[]{:S(2)}, u32[]{:S(2)}) %collective-permute-start) | collective-permute-done | bytes 65568 | tf_op jit(solution)/shard_map/while/body/eval_jaxpr/ppermute | solution.py:23
  175.2 5.6 %collective-permute-done = f32[512,32]{0,1:T(8,128)S(1)} collective-permute-done((f32[512,32]{0,1:T(8,128)S(1)}, f32[512,32]{0,1:T(8,128)S(1)}, u32[]{:S(2)}, u32[]{:S(2)}) %collective-permute-start) | collective-permute-done | bytes 65568 | tf_op jit(solution)/shard_map/while/body/eval_jaxpr/ppermute | solution.py:23
  183.0 14.1 %collective-permute-done = f32[512,32]{0,1:T(8,128)S(1)} collective-permute-done((f32[512,32]{0,1:T(8,128)S(1)}, f32[512,32]{0,1:T(8,128)S(1)}, u32[]{:S(2)}, u32[]{:S(2)}) %collective-permute-start) | collective-permute-done | bytes 65568 | tf_op jit(solution)/shard_map/while/body/eval_jaxpr/ppermute | solution.py:23
  199.2 5.6 %collective-permute-done = f32[512,32]{0,1:T(8,128)S(1)} collective-permute-done((f32[512,32]{0,1:T(8,128)S(1)}, f32[512,32]{0,1:T(8,128)S(1)}, u32[]{:S(2)}, u32[]{:S(2)}) %collective-permute-start) | collective-permute-done | bytes 65568 | tf_op jit(solution)/shard_map/while/body/eval_jaxpr/ppermute | solution.py:23
  207.0 12.6 %collective-permute-done = f32[512,32]{0,1:T(8,128)S(1)} collective-permute-done((f32[512,32]{0,1:T(8,128)S(1)}, f32[512,32]{0,1:T(8,128)S(1)}, u32[]{:S(2)}, u32[]{:S(2)}) %collective-permute-start) | collective-permute-done | bytes 65568 | tf_op jit(solution)/shard_map/while/body/eval_jaxpr/ppermute | solution.py:23
  221.7 86.4 %collective-permute-done = f32[512,32]{0,1:T(8,128)S(1)} collective-permute-done((f32[512,32]{0,1:T(8,128)S(1)}, f32[512,32]{0,1:T(8,128)S(1)}, u32[]{:S(2)}, u32[]{:S(2)}) %collective-permute-start) | collective-permute-done | bytes 65568 | tf_op jit(solution)/shard_map/while/body/eval_jaxpr/ppermute | solution.py:23
  308.1 12.4 %conditional.7 = (f32[512,32]{0,1:T(8,128)S(1)}, f32[4,512,32]{1,2,0:T(8,128)}) conditional(s32[]{:T(128)} %convert_element_type.27, () %tuple.153, (f32[4,512,32]{1,2,0:T(8,128)S(1)}, f32[4,512,512]{2,1,0:T(8,128)}, f32[512,32]{0,1:T(8,128)S(1)}) %tuple.154), branch_computations={%region_9.9_spmd, %region_10.12_spmd} | conditional | flops 100679680 | bytes 1836205 | solution.py:74
  308.8 11.7 %while.59 = (s32[]{:T(128)}, f32[512,32]{0,1:T(8,128)S(1)}, f32[4,512,32]{1,2,0:T(8,128)}, f32[4,512,32]{1,2,0:T(8,128)S(1)}, f32[4,512,512]{2,1,0:T(8,128)}, /*index=5*/s32[]{:T(128)}, s32[]{:T(128)}) while((s32[]{:T(128)}, f32[512,32]{0,1:T(8,128)S(1)}, f32[4,512,32]{1,2,0:T(8,128)}, f32[4,512,32]{1,2,0:T(8,128)S(1)}, ...), condition=%wide.region_12.11_spmd, body=%wide.region_11.10_spmd.sunk | while | flops 100679680 | bytes 1442905 | solution.py:53
  308.8 2.9 bitcast_dynamic-update-slice_fusion.4
  311.7 2.9 bitcast_dynamic-update-slice_fusion.4
  314.6 2.9 bitcast_dynamic-update-slice_fusion.4
  317.6 2.9 bitcast_dynamic-update-slice_fusion.4
  322.8 3.8 collective-permute-done
  328.4 3.4 all-to-all-start.1
  331.9 5.9 %all-to-all-done.1 = f32[4,1,16384]{2,1,0:T(1,128)S(1)} async-done(((f32[4,1,16384]{2,1,0:T(1,128)}), f32[4,1,16384]{2,1,0:T(1,128)S(1)}, u32[]{:S(2)}, u32[]{:S(2)}) %all-to-all-start.1) | async-done | bytes 262176 | tf_op jit(solution)/shard_map/all_to_all | solution.py:103
  341.9 4.5 %collective-permute-start.3 = (f32[1,128,128]{1,2,0:T(8,128)S(1)}, f32[1,128,128]{1,2,0:T(8,128)S(1)}, u32[]{:S(2)}, u32[]{:S(2)}) collective-permute-start(f32[1,128,128]{1,2,0:T(8,128)S(1)} %bitcast.61), channel_id=1, source_target_pairs={{0,4},{4,8},{8,12},{12,16},{16,20},{20,24},{24,28},{1,5},{5,9},{9,... | collective-permute-start | bytes 196616 | tf_op jit(solution)/shard_map/ppermute | solution.py:14
  349.9 3.1 collective-permute-start.5
  355.9 4.9 %collective-permute-start.11 = (f32[1,128,128]{1,2,0:T(8,128)S(1)}, f32[1,128,128]{1,2,0:T(8,128)S(1)}, u32[]{:S(2)}, u32[]{:S(2)}) collective-permute-start(f32[1,128,128]{1,2,0:T(8,128)S(1)} %get-tuple-element.502), channel_id=1, source_target_pairs={{0,4},{4,8},{8,12},{12,16},{16,20},{20,24},{24,28},{1,5},{5,9},{9,... | collective-permute-start | bytes 196616 | tf_op jit(solution)/shard_map/ppermute | solution.py:14
  362.2 5.7 %collective-permute-start.9 = (f32[6,1,128]{1,2,0:T(8,128)S(1)}, f32[6,1,128]{1,2,0:T(8,128)S(1)}, u32[]{:S(2)}, u32[]{:S(2)}) collective-permute-start(f32[6,1,128]{1,2,0:T(8,128)S(1)} %get-tuple-element.499), channel_id=1, source_target_pairs={{0,1},{1,2},{2,3},{4,5},{5,6},{6,7},{8,9},{9,10},{10,11},{12,13},{... | collective-permute-start | bytes 9224 | tf_op jit(solution)/shard_map/ppermute | solution.py:14
  369.5 5.3 %collective-permute-start.13 = (f32[6,1,128]{1,2,0:T(8,128)S(1)}, f32[6,1,128]{1,2,0:T(8,128)S(1)}, u32[]{:S(2)}, u32[]{:S(2)}) collective-permute-start(f32[6,1,128]{1,2,0:T(8,128)S(1)} %get-tuple-element.497), channel_id=1, source_target_pairs={{0,1},{1,2},{2,3},{4,5},{5,6},{6,7},{8,9},{9,10},{10,11},{12,13},{... | collective-permute-start | bytes 9224 | tf_op jit(solution)/shard_map/ppermute | solution.py:14
  378.5 45.9 %all-reduce.6 = (f32[]{:T(128)}, f32[]{:T(128)}, f32[]{:T(128)}, f32[]{:T(128)}, f32[]{:T(128)}, /*index=5*/f32[]{:T(128)}, f32[]{:T(128)}, f32[]{:T(128)}) all-reduce(f32[]{:T(128)} %get-tuple-element.434, f32[]{:T(128)} %multiply_reduce_fusion.8, f32[]{:T(128)} %get-tuple-element.433, ...), channel_id=1, replica_groups=mesh['layer'=8,'split'=4] {'layer','split'}, use_global_device_ids=true, to_apply=%region_17.18 | all-reduce | flops 8 | bytes 64 | tf_op jit(solution)/shard_map/psum | solution.py:106
  (136 shorter events, 62.6 us)
Async XLA Ops:
  7.2 40.1 %all-gather.2.cloned.1.call-start = ((), (), s32[]{:S(2)}) async-start(), calls=%async_computation.2 | async-start | bytes 5242880 | tf_op jit(solution)/shard_map/all_gather | solution.py:86
  9.7 14.2 %all-to-all-start = ((f32[4,128,128]{1,0,2:T(4,128)}), f32[4,128,128]{1,0,2:T(4,128)S(1)}, u32[]{:S(2)}, u32[]{:S(2)}) async-start(f32[4,128,128]{1,0,2:T(4,128)} %copy.44), calls=%async_computation | async-start | bytes 524288 | tf_op jit(solution)/shard_map/all_to_all | solution.py:87
  15.1 331.4 %collective-permute-start.6 = (f32[1,128,128]{1,2,0:T(8,128)S(1)}, f32[1,128,128]{1,2,0:T(8,128)S(1)}, u32[]{:S(2)}, u32[]{:S(2)}) collective-permute-start(f32[1,128,128]{1,2,0:T(8,128)S(1)} %get-tuple-element.507), channel_id=1, source_target_pairs={{4,0},{8,4},{12,8},{16,12},{20,16},{24,20},{28,24},{5,1},{9,5},{13... | collective-permute-start | bytes 196616 | tf_op jit(solution)/shard_map/ppermute | solution.py:15
  16.4 330.1 %collective-permute-start.7 = (f32[1,128,128]{1,2,0:T(8,128)S(1)}, f32[1,128,128]{1,2,0:T(8,128)S(1)}, u32[]{:S(2)}, u32[]{:S(2)}) collective-permute-start(f32[1,128,128]{1,2,0:T(8,128)S(1)} %get-tuple-element.506), channel_id=1, source_target_pairs={{0,4},{4,8},{8,12},{12,16},{16,20},{20,24},{24,28},{1,5},{5,9},{9,... | collective-permute-start | bytes 196616 | tf_op jit(solution)/shard_map/ppermute | solution.py:14
  59.0 3.3 collective-permute-start.1
  63.1 17.3 %collective-permute-start.1 = (f32[512,32]{0,1:T(8,128)S(1)}, f32[512,32]{0,1:T(8,128)S(1)}, u32[]{:S(2)}, u32[]{:S(2)}) collective-permute-start(f32[512,32]{0,1:T(8,128)S(1)} %get-tuple-element.643), channel_id=1, source_target_pairs={{0,4},{4,8},{8,12},{12,16},{16,20},{20,24},{24,28},{1,5},{5,9},{9,... | collective-permute-start | bytes 196616 | tf_op jit(solution)/shard_map/while/body/eval_jaxpr/ppermute | solution.py:23
  81.1 6.1 %collective-permute-start.1 = (f32[512,32]{0,1:T(8,128)S(1)}, f32[512,32]{0,1:T(8,128)S(1)}, u32[]{:S(2)}, u32[]{:S(2)}) collective-permute-start(f32[512,32]{0,1:T(8,128)S(1)} %get-tuple-element.643), channel_id=1, source_target_pairs={{0,4},{4,8},{8,12},{12,16},{16,20},{20,24},{24,28},{1,5},{5,9},{9,... | collective-permute-start | bytes 196616 | tf_op jit(solution)/shard_map/while/body/eval_jaxpr/ppermute | solution.py:23
  87.9 15.7 %collective-permute-start.1 = (f32[512,32]{0,1:T(8,128)S(1)}, f32[512,32]{0,1:T(8,128)S(1)}, u32[]{:S(2)}, u32[]{:S(2)}) collective-permute-start(f32[512,32]{0,1:T(8,128)S(1)} %get-tuple-element.643), channel_id=1, source_target_pairs={{0,4},{4,8},{8,12},{12,16},{16,20},{20,24},{24,28},{1,5},{5,9},{9,... | collective-permute-start | bytes 196616 | tf_op jit(solution)/shard_map/while/body/eval_jaxpr/ppermute | solution.py:23
  104.4 7.0 %collective-permute-start.1 = (f32[512,32]{0,1:T(8,128)S(1)}, f32[512,32]{0,1:T(8,128)S(1)}, u32[]{:S(2)}, u32[]{:S(2)}) collective-permute-start(f32[512,32]{0,1:T(8,128)S(1)} %get-tuple-element.643), channel_id=1, source_target_pairs={{0,4},{4,8},{8,12},{12,16},{16,20},{20,24},{24,28},{1,5},{5,9},{9,... | collective-permute-start | bytes 196616 | tf_op jit(solution)/shard_map/while/body/eval_jaxpr/ppermute | solution.py:23
  112.1 13.9 %collective-permute-start.1 = (f32[512,32]{0,1:T(8,128)S(1)}, f32[512,32]{0,1:T(8,128)S(1)}, u32[]{:S(2)}, u32[]{:S(2)}) collective-permute-start(f32[512,32]{0,1:T(8,128)S(1)} %get-tuple-element.643), channel_id=1, source_target_pairs={{0,4},{4,8},{8,12},{12,16},{16,20},{20,24},{24,28},{1,5},{5,9},{9,... | collective-permute-start | bytes 196616 | tf_op jit(solution)/shard_map/while/body/eval_jaxpr/ppermute | solution.py:23
  126.8 7.0 %collective-permute-start.1 = (f32[512,32]{0,1:T(8,128)S(1)}, f32[512,32]{0,1:T(8,128)S(1)}, u32[]{:S(2)}, u32[]{:S(2)}) collective-permute-start(f32[512,32]{0,1:T(8,128)S(1)} %get-tuple-element.643), channel_id=1, source_target_pairs={{0,4},{4,8},{8,12},{12,16},{16,20},{20,24},{24,28},{1,5},{5,9},{9,... | collective-permute-start | bytes 196616 | tf_op jit(solution)/shard_map/while/body/eval_jaxpr/ppermute | solution.py:23
  134.6 14.8 %collective-permute-start.1 = (f32[512,32]{0,1:T(8,128)S(1)}, f32[512,32]{0,1:T(8,128)S(1)}, u32[]{:S(2)}, u32[]{:S(2)}) collective-permute-start(f32[512,32]{0,1:T(8,128)S(1)} %get-tuple-element.643), channel_id=1, source_target_pairs={{0,4},{4,8},{8,12},{12,16},{16,20},{20,24},{24,28},{1,5},{5,9},{9,... | collective-permute-start | bytes 196616 | tf_op jit(solution)/shard_map/while/body/eval_jaxpr/ppermute | solution.py:23
  150.1 7.4 %collective-permute-start = (f32[512,32]{0,1:T(8,128)S(1)}, f32[512,32]{0,1:T(8,128)S(1)}, u32[]{:S(2)}, u32[]{:S(2)}) collective-permute-start(f32[512,32]{0,1:T(8,128)S(1)} %get-tuple-element.651), channel_id=1, source_target_pairs={{4,0},{8,4},{12,8},{16,12},{20,16},{24,20},{28,24},{5,1},{9,5},{13... | collective-permute-start | bytes 196616 | tf_op jit(solution)/shard_map/while/body/eval_jaxpr/ppermute | solution.py:23
  158.2 14.9 %collective-permute-start = (f32[512,32]{0,1:T(8,128)S(1)}, f32[512,32]{0,1:T(8,128)S(1)}, u32[]{:S(2)}, u32[]{:S(2)}) collective-permute-start(f32[512,32]{0,1:T(8,128)S(1)} %get-tuple-element.651), channel_id=1, source_target_pairs={{4,0},{8,4},{12,8},{16,12},{20,16},{24,20},{28,24},{5,1},{9,5},{13... | collective-permute-start | bytes 196616 | tf_op jit(solution)/shard_map/while/body/eval_jaxpr/ppermute | solution.py:23
  173.8 7.0 %collective-permute-start = (f32[512,32]{0,1:T(8,128)S(1)}, f32[512,32]{0,1:T(8,128)S(1)}, u32[]{:S(2)}, u32[]{:S(2)}) collective-permute-start(f32[512,32]{0,1:T(8,128)S(1)} %get-tuple-element.651), channel_id=1, source_target_pairs={{4,0},{8,4},{12,8},{16,12},{20,16},{24,20},{28,24},{5,1},{9,5},{13... | collective-permute-start | bytes 196616 | tf_op jit(solution)/shard_map/while/body/eval_jaxpr/ppermute | solution.py:23
  181.6 15.5 %collective-permute-start = (f32[512,32]{0,1:T(8,128)S(1)}, f32[512,32]{0,1:T(8,128)S(1)}, u32[]{:S(2)}, u32[]{:S(2)}) collective-permute-start(f32[512,32]{0,1:T(8,128)S(1)} %get-tuple-element.651), channel_id=1, source_target_pairs={{4,0},{8,4},{12,8},{16,12},{20,16},{24,20},{28,24},{5,1},{9,5},{13... | collective-permute-start | bytes 196616 | tf_op jit(solution)/shard_map/while/body/eval_jaxpr/ppermute | solution.py:23
  197.8 7.0 %collective-permute-start = (f32[512,32]{0,1:T(8,128)S(1)}, f32[512,32]{0,1:T(8,128)S(1)}, u32[]{:S(2)}, u32[]{:S(2)}) collective-permute-start(f32[512,32]{0,1:T(8,128)S(1)} %get-tuple-element.651), channel_id=1, source_target_pairs={{4,0},{8,4},{12,8},{16,12},{20,16},{24,20},{28,24},{5,1},{9,5},{13... | collective-permute-start | bytes 196616 | tf_op jit(solution)/shard_map/while/body/eval_jaxpr/ppermute | solution.py:23
  205.6 14.0 %collective-permute-start = (f32[512,32]{0,1:T(8,128)S(1)}, f32[512,32]{0,1:T(8,128)S(1)}, u32[]{:S(2)}, u32[]{:S(2)}) collective-permute-start(f32[512,32]{0,1:T(8,128)S(1)} %get-tuple-element.651), channel_id=1, source_target_pairs={{4,0},{8,4},{12,8},{16,12},{20,16},{24,20},{28,24},{5,1},{9,5},{13... | collective-permute-start | bytes 196616 | tf_op jit(solution)/shard_map/while/body/eval_jaxpr/ppermute | solution.py:23
  220.3 87.8 %collective-permute-start = (f32[512,32]{0,1:T(8,128)S(1)}, f32[512,32]{0,1:T(8,128)S(1)}, u32[]{:S(2)}, u32[]{:S(2)}) collective-permute-start(f32[512,32]{0,1:T(8,128)S(1)} %get-tuple-element.651), channel_id=1, source_target_pairs={{4,0},{8,4},{12,8},{16,12},{20,16},{24,20},{28,24},{5,1},{9,5},{13... | collective-permute-start | bytes 196616 | tf_op jit(solution)/shard_map/while/body/eval_jaxpr/ppermute | solution.py:23
  320.5 6.2 %collective-permute-start = (f32[512,32]{0,1:T(8,128)S(1)}, f32[512,32]{0,1:T(8,128)S(1)}, u32[]{:S(2)}, u32[]{:S(2)}) collective-permute-start(f32[512,32]{0,1:T(8,128)S(1)} %get-tuple-element.651), channel_id=1, source_target_pairs={{4,0},{8,4},{12,8},{16,12},{20,16},{24,20},{28,24},{5,1},{9,5},{13... | collective-permute-start | bytes 196616 | tf_op jit(solution)/shard_map/while/body/eval_jaxpr/ppermute | solution.py:23
  328.4 9.4 %all-to-all-start.1 = ((f32[4,1,16384]{2,1,0:T(1,128)}), f32[4,1,16384]{2,1,0:T(1,128)S(1)}, u32[]{:S(2)}, u32[]{:S(2)}) async-start(f32[4,1,16384]{2,1,0:T(1,128)} %reshape.6), calls=%async_computation.1 | async-start | bytes 524288 | tf_op jit(solution)/shard_map/all_to_all | solution.py:103
  340.6 6.3 %collective-permute-start.2 = (f32[1,128,128]{1,2,0:T(8,128)S(1)}, f32[1,128,128]{1,2,0:T(8,128)S(1)}, u32[]{:S(2)}, u32[]{:S(2)}) collective-permute-start(f32[1,128,128]{1,2,0:T(8,128)S(1)} %bitcast.60), channel_id=1, source_target_pairs={{4,0},{8,4},{12,8},{16,12},{20,16},{24,20},{28,24},{5,1},{9,5},{13... | collective-permute-start | bytes 196616 | tf_op jit(solution)/shard_map/ppermute | solution.py:15
  341.9 6.4 %collective-permute-start.3 = (f32[1,128,128]{1,2,0:T(8,128)S(1)}, f32[1,128,128]{1,2,0:T(8,128)S(1)}, u32[]{:S(2)}, u32[]{:S(2)}) collective-permute-start(f32[1,128,128]{1,2,0:T(8,128)S(1)} %bitcast.61), channel_id=1, source_target_pairs={{0,4},{4,8},{8,12},{12,16},{16,20},{20,24},{24,28},{1,5},{5,9},{9,... | collective-permute-start | bytes 196616 | tf_op jit(solution)/shard_map/ppermute | solution.py:14
  348.6 4.4 %collective-permute-start.4 = (f32[6,1,128]{1,2,0:T(8,128)S(1)}, f32[6,1,128]{1,2,0:T(8,128)S(1)}, u32[]{:S(2)}, u32[]{:S(2)}) collective-permute-start(f32[6,1,128]{1,2,0:T(8,128)S(1)} %get-tuple-element.500), channel_id=1, source_target_pairs={{1,0},{2,1},{3,2},{5,4},{6,5},{7,6},{9,8},{10,9},{11,10},{13,12},{... | collective-permute-start | bytes 9224 | tf_op jit(solution)/shard_map/ppermute | solution.py:15
  349.9 4.4 collective-permute-start.5
  354.6 13.4 %collective-permute-start.10 = (f32[1,128,128]{1,2,0:T(8,128)S(1)}, f32[1,128,128]{1,2,0:T(8,128)S(1)}, u32[]{:S(2)}, u32[]{:S(2)}) collective-permute-start(f32[1,128,128]{1,2,0:T(8,128)S(1)} %get-tuple-element.503), channel_id=1, source_target_pairs={{4,0},{8,4},{12,8},{16,12},{20,16},{24,20},{28,24},{5,1},{9,5},{13... | collective-permute-start | bytes 196616 | tf_op jit(solution)/shard_map/ppermute | solution.py:15
  355.9 12.1 %collective-permute-start.11 = (f32[1,128,128]{1,2,0:T(8,128)S(1)}, f32[1,128,128]{1,2,0:T(8,128)S(1)}, u32[]{:S(2)}, u32[]{:S(2)}) collective-permute-start(f32[1,128,128]{1,2,0:T(8,128)S(1)} %get-tuple-element.502), channel_id=1, source_target_pairs={{0,4},{4,8},{8,12},{12,16},{16,20},{20,24},{24,28},{1,5},{5,9},{9,... | collective-permute-start | bytes 196616 | tf_op jit(solution)/shard_map/ppermute | solution.py:14
  360.9 13.9 %collective-permute-start.8 = (f32[6,1,128]{1,2,0:T(8,128)S(1)}, f32[6,1,128]{1,2,0:T(8,128)S(1)}, u32[]{:S(2)}, u32[]{:S(2)}) collective-permute-start(f32[6,1,128]{1,2,0:T(8,128)S(1)} %get-tuple-element.498), channel_id=1, source_target_pairs={{1,0},{2,1},{3,2},{5,4},{6,5},{7,6},{9,8},{10,9},{11,10},{13,12},{... | collective-permute-start | bytes 9224 | tf_op jit(solution)/shard_map/ppermute | solution.py:15
  362.2 12.6 %collective-permute-start.9 = (f32[6,1,128]{1,2,0:T(8,128)S(1)}, f32[6,1,128]{1,2,0:T(8,128)S(1)}, u32[]{:S(2)}, u32[]{:S(2)}) collective-permute-start(f32[6,1,128]{1,2,0:T(8,128)S(1)} %get-tuple-element.499), channel_id=1, source_target_pairs={{0,1},{1,2},{2,3},{4,5},{5,6},{6,7},{8,9},{9,10},{10,11},{12,13},{... | collective-permute-start | bytes 9224 | tf_op jit(solution)/shard_map/ppermute | solution.py:14
  368.2 6.7 %collective-permute-start.12 = (f32[6,1,128]{1,2,0:T(8,128)S(1)}, f32[6,1,128]{1,2,0:T(8,128)S(1)}, u32[]{:S(2)}, u32[]{:S(2)}) collective-permute-start(f32[6,1,128]{1,2,0:T(8,128)S(1)} %get-tuple-element.496), channel_id=1, source_target_pairs={{1,0},{2,1},{3,2},{5,4},{6,5},{7,6},{9,8},{10,9},{11,10},{13,12},{... | collective-permute-start | bytes 9224 | tf_op jit(solution)/shard_map/ppermute | solution.py:15
  369.5 6.6 %collective-permute-start.13 = (f32[6,1,128]{1,2,0:T(8,128)S(1)}, f32[6,1,128]{1,2,0:T(8,128)S(1)}, u32[]{:S(2)}, u32[]{:S(2)}) collective-permute-start(f32[6,1,128]{1,2,0:T(8,128)S(1)} %get-tuple-element.497), channel_id=1, source_target_pairs={{0,1},{1,2},{2,3},{4,5},{5,6},{6,7},{8,9},{9,10},{10,11},{12,13},{... | collective-permute-start | bytes 9224 | tf_op jit(solution)/shard_map/ppermute | solution.py:14
Sparse Core Ops, SparseCore 0:
  9.5 37.7 all-gather.1
where the time goes:
time: 441 us; the launch traced here: 438 us
  waiting for transfers between devices  195 us (44%)
  starting transfers between devices  124 us (28%)
  blocking collectives  45.9 us (10%)
  matrix products  23.3 us (5%)
  local copies, waits for them, and re-layouts  21 us (5%)
  between operations  20.8 us (5%)
  other arithmetic  8.15 us (2%)
    ppermute x16, waiting for transfers between devices, from_behind(): return lax.ppermute(block, axis, route)  161 us
    ppermute x16, starting transfers between devices, from_behind(): return lax.ppermute(block, axis, route)  80.1 us
    psum x1, blocking collectives, per_device(): lax.psum((jnp.sum(right_side * right_side), jnp.sum(right_side * image),...  45.9 us
    ppermute x6, starting transfers between devices, with_halo(): before = lax.ppermute(last, axis, up)  28.1 us
    all_gather x1, waiting for transfers between devices, per_device(): matrices = lax.all_gather(inverses, 'split', axis=2, tiled=True)  23.4 us
    dot_general x4, matrix products, down_advance(): state = jnp.dot(matrix, source + state, precision=lax.Precision.HIGHEST)  11.7 us
    dot_general x4, matrix products, up_advance(): state = below + jnp.dot(matrix, state, precision=lax.Precision.HIGHEST)  11.7 us
    another operation x31, local copies, waits for them, and re-layouts  11 us
  transfers between devices with their start and end apart: 31, of which 21 were waited for; matrix products, arithmetic and copies ran while one was open for 11% of the time, Pallas kernels for 0%

commit v1 on v0

v1 whole, which is shorter than its diff:
```python
import jax
import jax.numpy as jnp
from jax import lax
from jax.experimental import pallas as pl
from jax.experimental.pallas import tpu as pltpu
from jax.sharding import PartitionSpec as P

F32 = jnp.float32
BF16 = jnp.bfloat16
EDGE = 8


def split_parts(x):
    high = x.astype(BF16)
    return high, (x - high.astype(F32)).astype(BF16)


def dot_nt(a, b):
    return lax.dot_general(a, b, (((1,), (1,)), ((), ())), preferred_element_type=F32)


def apply_rows(rows, high, low):
    n = rows.shape[0]
    a, b = split_parts(rows)
    both = dot_nt(jnp.concatenate([a, b], axis=0), high)
    return both[:n] + both[n:] + dot_nt(a, low)


def product(a, b):
    ah, al = a
    bh, bl = b
    out = jnp.dot(ah, bh, preferred_element_type=F32)
    out = out + jnp.dot(ah, bl, preferred_element_type=F32)
    return out + jnp.dot(al, bh, preferred_element_type=F32)


def chain_product(pairs):
    while len(pairs) > 1:
        merged = [
            split_parts(product(pairs[i], pairs[i + 1])) for i in range(0, len(pairs) - 1, 2)
        ]
        if len(pairs) % 2:
            merged.append(pairs[-1])
        pairs = merged
    return pairs[0]


def call(body, out, *args, smem=0):
    vm = pl.BlockSpec(memory_space=pltpu.VMEM)
    specs = [pl.BlockSpec(memory_space=pltpu.SMEM)] * smem + [vm] * (len(args) - smem)
    shapes = [jax.ShapeDtypeStruct(s, d) for s, d in out]
    return pl.pallas_call(
        body, out_shape=shapes, in_specs=specs, out_specs=[vm] * len(shapes), name=body.__name__
    )(*args)


def prepare(place, *refs):
    count = place.shape[0]
    blocks = refs[:count]
    pieces, mh, ml, ph, plo, qh, qlo, tail, cols = refs[count:]
    planes, nx, width = blocks[0].shape
    for j in range(count):
        at = pl.multiple_of(place[j] * width, width)
        for k in range(planes):
            high, low = split_parts(blocks[j][k])
            mh[k, :, pl.ds(at, width)] = high
            ml[k, :, pl.ds(at, width)] = low
        cols[:, :, j * width : (j + 1) * width] = pieces[j]
    state = cols[0]
    for k in range(planes):
        if k:
            state = state + cols[k]
        state = apply_rows(state, mh[k], ml[k])
    tail[...] = state
    order = [(mh[k], ml[k]) for k in range(planes)]
    ph[...], plo[...] = chain_product(order[::-1])
    qh[...], qlo[...] = chain_product(order)


def hop(held, came, base, high, low, now, out):
    state = held[...] + came[...]
    now[...] = state
    out[...] = base[...] + apply_rows(state, high[...], low[...])


def turn(held, came, cols, mh, ml, lower, top):
    planes = cols.shape[0]
    state = held[...] + came[...]
    for k in range(planes):
        state = apply_rows(cols[k] + state, mh[k], ml[k])
        lower[k] = state
    for k in reversed(range(planes - 1)):
        state = lower[k] + apply_rows(state, mh[k], ml[k])
    top[...] = state


def rise(held, came, lower, mh, ml, direction, now):
    planes = lower.shape[0]
    state = held[...] + came[...]
    now[...] = state
    for k in reversed(range(planes)):
        state = lower[k] + apply_rows(state, mh[k], ml[k])
        direction[k] = state


def pack(direction, behind, above, ahead, out, tall):
    planes, ny, nx = direction.shape
    extended = jnp.concatenate([behind[...], direction[...], above[...][None], ahead[...]], axis=0)
    flat = extended.reshape((planes + 4) * ny, nx)
    tall[:EDGE] = jnp.zeros((EDGE, tall.shape[1]), F32)
    tall[EDGE + nx :] = jnp.zeros((EDGE, tall.shape[1]), F32)
    tall[EDGE : EDGE + nx] = flat.T
    count = out.shape[0]
    width = nx // count
    for j in range(count):
        out[j] = tall[j * width : j * width + width + 2 * EDGE]


def plane_stencil(below, here, above, diagonal):
    rows, ny = here.shape
    lane = lax.broadcasted_iota(jnp.int32, here.shape, 1)
    beside = below + above + pltpu.roll(here, 1, 0) + pltpu.roll(here, rows - 1, 0)
    beside = beside + jnp.where(lane > 0, pltpu.roll(here, 1, 1), 0.0)
    beside = beside + jnp.where(lane < ny - 1, pltpu.roll(here, ny - 1, 1), 0.0)
    return (6.0 + diagonal) * here - beside


def apply_rhs(extended, out):
    planes = out.shape[0]
    for k in range(planes):
        value = plane_stencil(
            extended[0, k], extended[0, k + 1], extended[0, k + 2], extended[1, k + 1]
        )
        out[k] = value[EDGE:-EDGE]


def images(where, recv, extended, applied_rhs, direction, image, applied_image, sums):
    planes = direction.shape[0]
    count, rows, packed = recv.shape
    part = packed // (planes + 4)
    depth = [
        jnp.concatenate([recv[j, :, p * part : (p + 1) * part] for j in range(count)], axis=1)
        for p in range(planes + 4)
    ]
    row = lax.broadcasted_iota(jnp.int32, depth[0].shape, 0) + where[0]
    inside_x = jnp.logical_and(row >= 0, row < where[2])
    made = {}
    for p in range(1, planes + 3):
        value = plane_stencil(depth[p - 1], depth[p], depth[p + 1], extended[1, p - 1])
        at = where[1] + p
        inside_z = jnp.logical_and(at >= 0, at < where[3])
        made[p] = jnp.where(jnp.logical_and(inside_x, inside_z), value, 0.0)
    totals = [jnp.zeros((EDGE, depth[0].shape[1]), F32) for _ in range(8)]
    for k in range(planes):
        p = k + 2
        twice = plane_stencil(made[p - 1], made[p], made[p + 1], extended[1, k + 1])[EDGE:-EDGE]
        once = made[p][EDGE:-EDGE]
        source = extended[0, k + 1][EDGE:-EDGE]
        about = applied_rhs[k]
        direction[k] = depth[p][EDGE:-EDGE]
        image[k] = once
        applied_image[k] = twice
        terms = (
            source * source,
            source * once,
            about * source,
            about * once + twice * source,
            twice * once,
            about * about,
            about * twice,
            twice * twice,
        )
        for i, term in enumerate(terms):
            totals[i] = totals[i] + jnp.sum(term.reshape(-1, EDGE, term.shape[1]), axis=0)
    lane = lax.broadcasted_iota(jnp.int32, sums.shape, 1)
    line = jnp.zeros(sums.shape, F32)
    for i, total in enumerate(totals):
        line = jnp.where(lane == i, jnp.sum(total), line)
    sums[...] = line


def finish(every, direction, image, applied_image, right_side, applied_rhs, solved, residual):
    total = jnp.sum(every[...], axis=0, keepdims=True)
    lane = lax.broadcasted_iota(jnp.int32, total.shape, 1)

    def pick(i):
        return jnp.sum(jnp.where(lane == i, total, 0.0), axis=1, keepdims=True)

    rr, ri, ar, cross, aii, arar, arai, aiai = [pick(i) for i in range(8)]
    alpha = rr / ri
    upper = ar - alpha * cross + alpha * alpha * aii
    under = arar - 2.0 * alpha * arai + alpha * alpha * aiai
    omega = upper / under
    for k in range(direction.shape[0]):
        middle = right_side[k] - alpha * image[k]
        tangent = applied_rhs[k] - alpha * applied_image[k]
        solved[k] = alpha * direction[k] + omega * middle
        residual[k] = middle - omega * tangent


def neighbours(x, axis):
    size = lax.axis_size(axis)
    up = [(i, i + 1) for i in range(size - 1)]
    down = [(i + 1, i) for i in range(size - 1)]
    return up, down


def per_device(right_side, diagonal, inverses):
    splits = lax.axis_size("split")
    depth = lax.axis_size("layer")
    own = lax.axis_index("split")
    layer = lax.axis_index("layer")
    planes, width, ny = right_side.shape
    nx = inverses.shape[1]
    part = ny // splits

    blocks = [inverses]
    offsets = [0]
    step = splits // 2
    while step:
        route = [(i, i ^ step) for i in range(splits)]
        blocks = blocks + [lax.ppermute(b, "split", route) for b in blocks]
        offsets = offsets + [o ^ step for o in offsets]
        step //= 2
    place = jnp.stack([own ^ o for o in offsets]).astype(jnp.int32)

    turned = jnp.swapaxes(right_side, 1, 2).reshape(planes, splits, part, width)
    pieces = lax.all_to_all(
        jnp.swapaxes(turned, 0, 1), "split", split_axis=0, concat_axis=0, tiled=True
    )

    pair = jnp.stack([right_side, diagonal])
    up, down = neighbours(pair, "layer")
    before = lax.ppermute(pair[:, -1:], "layer", up)
    after = lax.ppermute(pair[:, :1], "layer", down)
    pair = jnp.concatenate([before, pair, after], axis=1)
    up, down = neighbours(pair, "split")
    before = lax.ppermute(pair[:, :, -EDGE:], "split", up)
    after = lax.ppermute(pair[:, :, :EDGE], "split", down)
    pair = jnp.concatenate([before, pair, after], axis=2)
    (applied_rhs,) = call(apply_rhs, [(right_side.shape, F32)], pair)

    column = (part, nx)
    square = (nx, nx)
    stack = (planes,) + column
    mh, ml, ph, plo, qh, qlo, tail, cols = call(
        prepare,
        [((planes,) + square, BF16)] * 2 + [(square, BF16)] * 4 + [(column, F32), (stack, F32)],
        place,
        *blocks,
        pieces,
        smem=1,
    )

    zero = jnp.zeros(column, F32)
    held, out = zero, tail
    for t in range(depth - 1):
        came = lax.ppermute(out, "layer", [(t, t + 1)])
        if t < depth - 2:
            held, out = call(hop, [(column, F32)] * 2, held, came, tail, ph, plo)
    lower, top = call(turn, [(stack, F32), (column, F32)], held, came, cols, mh, ml)

    held, out = zero, top
    for t in range(depth - 1):
        came = lax.ppermute(out, "layer", [(depth - 1 - t, depth - 2 - t)])
        if t < depth - 2:
            held, out = call(hop, [(column, F32)] * 2, held, came, top, qh, qlo)
    swept, above = call(rise, [(stack, F32), (column, F32)], held, came, lower, mh, ml)

    up, down = neighbours(swept, "layer")
    behind = lax.ppermute(swept[-2:], "layer", up)
    ahead = lax.ppermute(swept[1:2], "layer", down)
    rows = width + 2 * EDGE
    packed = (planes + 4) * part
    vm = pl.BlockSpec(memory_space=pltpu.VMEM)
    windows = pl.pallas_call(
        pack,
        out_shape=jax.ShapeDtypeStruct((splits, rows, packed), F32),
        in_specs=[vm] * 4,
        out_specs=vm,
        scratch_shapes=[pltpu.VMEM((nx + 2 * EDGE, packed), F32)],
        name="pack",
    )(swept, behind, above, ahead)
    recv = lax.all_to_all(windows, "split", split_axis=0, concat_axis=0, tiled=True)

    where = jnp.stack(
        [own * width - EDGE, layer * planes - 2, splits * width, depth * planes]
    ).astype(jnp.int32)
    block = (right_side.shape, F32)
    total = depth * splits
    direction, image, applied_image, sums = call(
        images, [block] * 3 + [((total, ny), F32)], where, recv, pair, applied_rhs, smem=1
    )
    every = lax.all_to_all(sums, ("layer", "split"), split_axis=0, concat_axis=0, tiled=True)
    return tuple(
        call(
            finish, [block] * 2, every, direction, image, applied_image, right_side, applied_rhs
        )
    )


def solution(mesh):
    placed = (P("layer", "split", None), P("layer", "split", None), P("layer", None, "split"))
    return jax.shard_map(
        per_device,
        mesh=mesh,
        in_specs=placed,
        out_specs=(P("layer", "split", None), P("layer", "split", None)),
        check_vma=False,
    )
```

time: 441 us -> 217 us (0.49)
  waiting for transfers between devices: 195 us -> 89.8 us
  starting transfers between devices: 124 us -> 35.1 us
  Pallas kernels: 0 us -> 58.3 us
  blocking collectives: 45.9 us -> 13.7 us
  matrix products: 23.3 us -> 0 us
  between operations: 20.8 us -> 1.15 us
  other arithmetic: 8.15 us -> 2.24 us
  local copies, waits for them, and re-layouts: 21 us -> 16 us
    ppermute x28 -> x23, starting transfers between devices: 116 us -> 28.2 us  [the longest x7 7.52 us: per_device(): came = lax.ppermute(out, 'layer', [(t, t + 1)])]
    ppermute x28 -> x23, waiting for transfers between devices: 165 us -> 84.4 us  [the longest x7 56.5 us: per_device(): came = lax.ppermute(out, 'layer', [(depth - 1 - t, depth - 2 - t)])]
    pallas_call x0 -> x19, Pallas kernels: none -> 58.3 us  [the longest x18 56.3 us: call(): pl.pallas_call(body, out_shape=shapes, in_specs=specs, out_specs=[vm] * l...]
    psum x1 -> x0, blocking collectives: 45.9 us -> none  [per_device(): lax.psum((jnp.sum(right_side * right_side), jnp.sum(right_side * image),...]
    all_gather x1 -> x0, waiting for transfers between devices: 23.4 us -> none  [per_device(): matrices = lax.all_gather(inverses, 'split', axis=2, tiled=True)]
    dot_general x8 -> x0, matrix products: 23.3 us -> none  [the longest x4 11.7 us: down_advance(): state = jnp.dot(matrix, source + state, precision=lax.Precision.HIGHEST)]
    all_to_all x0 -> x1, blocking collectives: none -> 13.7 us  [per_device(): lax.all_to_all(sums, ('layer', 'split'), split_axis=0, concat_axis=0, til...]
    another operation x31 -> x0, local copies, waits for them, and re-layouts: 11 us -> none
  transfers between devices with their start and end apart: 31 -> 25, of which waited for: 21 -> 5; matrix products, arithmetic and copies ran while one was open for 11% -> 2% of each run, Pallas kernels for 0% -> 2%
where the time goes in v1:
time: 217 us; the launch traced here: 216 us
  waiting for transfers between devices  89.8 us (41%)
  Pallas kernels  58.3 us (27%)
  starting transfers between devices  35.1 us (16%)
  local copies, waits for them, and re-layouts  16 us (7%)
  blocking collectives  13.7 us (6%)
  other arithmetic  2.24 us (1%)
    ppermute x7, waiting for transfers between devices, per_device(): came = lax.ppermute(out, 'layer', [(depth - 1 - t, depth - 2 - t)])  56.5 us
    pallas_call x18, Pallas kernels, call(): pl.pallas_call(body, out_shape=shapes, in_specs=specs, out_specs=[vm] * l...  56.3 us
    ppermute x3, waiting for transfers between devices, per_device(): blocks = blocks + [lax.ppermute(b, 'split', route) for b in blocks]  23.4 us
    all_to_all x1, blocking collectives, per_device(): lax.all_to_all(sums, ('layer', 'split'), split_axis=0, concat_axis=0, til...  13.7 us
    unnamed x47, local copies, waits for them, and re-layouts  12.9 us
    ppermute x7, starting transfers between devices, per_device(): came = lax.ppermute(out, 'layer', [(t, t + 1)])  7.52 us
    all_to_all x1, waiting for transfers between devices, per_device(): lax.all_to_all(jnp.swapaxes(turned, 0, 1), 'split', split_axis=0, concat_...  5.37 us
    ppermute x7, starting transfers between devices, per_device(): came = lax.ppermute(out, 'layer', [(depth - 1 - t, depth - 2 - t)])  5.2 us
  transfers between devices with their start and end apart: 25, of which 5 were waited for; matrix products, arithmetic and copies ran while one was open for 2% of the time, Pallas kernels for 2%

profile of v1, /device:TPU:0, one launch (start us, length us, event | category | flops | bytes accessed | tf_op | source)
XLA Modules:
  0.0 216.4 jit_solution(16609930258694500556)
XLA Ops:
  0.6 3.1 %collective-permute-start = (f32[4,512,128]{2,1,0:T(8,128)}, f32[4,512,128]{2,1,0:T(8,128)S(1)}, u32[]{:S(2)}, u32[]{:S(2)}) collective-permute-start(f32[4,512,128]{2,1,0:T(8,128)} %refs_0_.1), channel_id=1, source_target_pairs={{0,2},{1,3},{2,0},{3,1},{4,6},{5,7},{6,4},{7,5},{8,10},{9,11},{10,... | collective-permute-start | bytes 3145736 | tf_op jit(solution)/shard_map/ppermute | solution.py:222
  3.7 23.4 %collective-permute-done.refs_1_ = f32[4,512,128]{2,1,0:T(8,128)S(1)} collective-permute-done((f32[4,512,128]{2,1,0:T(8,128)}, f32[4,512,128]{2,1,0:T(8,128)S(1)}, u32[]{:S(2)}, u32[]{:S(2)}) %collective-permute-start) | collective-permute-done | bytes 1048608 | tf_op jit(solution)/shard_map/ppermute | solution.py:222
  27.1 1.2 copy.7
  28.3 0.7 copy.11
  29.0 3.4 %all-to-all-start = ((f32[4,4,32,128]{3,2,1,0:T(8,128)}), f32[4,4,32,128]{3,2,1,0:T(8,128)S(1)}, u32[]{:S(2)}, u32[]{:S(2)}) async-start(f32[4,4,32,128]{3,2,1,0:T(8,128)} %bitcast.24), calls=%async_computation | async-start | bytes 524288 | tf_op jit(solution)/shard_map/all_to_all | solution.py:228
  33.1 5.4 %all-to-all-done.refs_4_ = f32[4,4,32,128]{3,2,1,0:T(8,128)S(1)} async-done(((f32[4,4,32,128]{3,2,1,0:T(8,128)}), f32[4,4,32,128]{3,2,1,0:T(8,128)S(1)}, u32[]{:S(2)}, u32[]{:S(2)}) %all-to-all-start) | async-done | bytes 262176 | tf_op jit(solution)/shard_map/all_to_all | solution.py:228
  38.4 0.7 copy-done.6
  39.5 1.0 copy-done.5
  40.5 10.8 %prepare.1 = (bf16[4,512,512]{2,1,0:T(8,128)(2,1)}, bf16[4,512,512]{2,1,0:T(8,128)(2,1)}, bf16[512,512]{1,0:T(8,128)(2,1)}, bf16[512,512]{1,0:T(8,128)(2,1)}, bf...) custom-call(s32[4]{0:T(128)} %pad_add_fusion.1.place, ...), custom_call_target="tpu_custom_call" | custom-call | tf_op jit(solution)/shard_map/prepare/pallas_call | solution.py:52
  51.3 3.6 %collective-permute-start.3 = (f32[32,512]{1,0:T(8,128)}, f32[32,512]{1,0:T(8,128)S(1)}, u32[]{:S(2)}, u32[]{:S(2)}) collective-permute-start(f32[32,512]{1,0:T(8,128)} %get-tuple-element.42.base), channel_id=1, source_target_pairs={{0,4},{1,5},{2,6},{3,7}} | collective-permute-start | bytes 196616 | tf_op jit(solution)/shard_map/ppermute | solution.py:258
  55.0 2.2 %collective-permute-done.3.came = f32[32,512]{1,0:T(8,128)S(1)} collective-permute-done((f32[32,512]{1,0:T(8,128)}, f32[32,512]{1,0:T(8,128)S(1)}, u32[]{:S(2)}, u32[]{:S(2)}) %collective-permute-start.3) | collective-permute-done | bytes 65568 | tf_op jit(solution)/shard_map/ppermute | solution.py:258
  57.8 2.3 %hop.12 = (f32[32,512]{1,0:T(8,128)}, f32[32,512]{1,0:T(8,128)}) custom-call(f32[32,512]{1,0:T(8,128)} %broadcast_in_dim.3.held, f32[32,512]{1,0:T(8,128)} %copy-done.21, f32[32,512]{1,0:T(8,128)} %get-tuple-element.42.base, bf16[512,512]{1,0:T(8,128)(2,1)} %get-tuple-element.43.high, bf16[512,512]{1,0:T(8,128)(2,1)} %get-tuple-element.44.low), custom_call_target="tpu_custom_call" | custom-call | tf_op jit(solution)/shard_map/hop/pallas_call | solution.py:52
  61.4 2.3 %hop.13 = (f32[32,512]{1,0:T(8,128)}, f32[32,512]{1,0:T(8,128)}) custom-call(f32[32,512]{1,0:T(8,128)} %get-tuple-element.45.held, f32[32,512]{1,0:T(8,128)} %copy-done.13, f32[32,512]{1,0:T(8,128)} %get-tuple-element.42.base, bf16[512,512]{1,0:T(8,128)(2,1)} %get-tuple-element.43.high, bf16[512,512]{1,0:T(8,128)(2,1)} %get-tuple-element.44.low), custom_call_target="tpu_custom_call" | custom-call | tf_op jit(solution)/shard_map/hop/pallas_call | solution.py:52
  65.0 2.3 %hop.14 = (f32[32,512]{1,0:T(8,128)}, f32[32,512]{1,0:T(8,128)}) custom-call(f32[32,512]{1,0:T(8,128)} %get-tuple-element.47.held, f32[32,512]{1,0:T(8,128)} %copy-done.14, f32[32,512]{1,0:T(8,128)} %get-tuple-element.42.base, bf16[512,512]{1,0:T(8,128)(2,1)} %get-tuple-element.43.high, bf16[512,512]{1,0:T(8,128)(2,1)} %get-tuple-element.44.low), custom_call_target="tpu_custom_call" | custom-call | tf_op jit(solution)/shard_map/hop/pallas_call | solution.py:52
  67.4 0.7 collective-permute-start.6
  68.7 2.3 %hop.15 = (f32[32,512]{1,0:T(8,128)}, f32[32,512]{1,0:T(8,128)}) custom-call(f32[32,512]{1,0:T(8,128)} %get-tuple-element.49.held, f32[32,512]{1,0:T(8,128)} %copy-done.15, f32[32,512]{1,0:T(8,128)} %get-tuple-element.42.base, bf16[512,512]{1,0:T(8,128)(2,1)} %get-tuple-element.43.high, bf16[512,512]{1,0:T(8,128)(2,1)} %get-tuple-element.44.low), custom_call_target="tpu_custom_call" | custom-call | tf_op jit(solution)/shard_map/hop/pallas_call | solution.py:52
  71.0 0.7 collective-permute-start.7
  72.3 2.3 %hop.16 = (f32[32,512]{1,0:T(8,128)}, f32[32,512]{1,0:T(8,128)}) custom-call(f32[32,512]{1,0:T(8,128)} %get-tuple-element.51.held, f32[32,512]{1,0:T(8,128)} %copy-done.16, f32[32,512]{1,0:T(8,128)} %get-tuple-element.42.base, bf16[512,512]{1,0:T(8,128)(2,1)} %get-tuple-element.43.high, bf16[512,512]{1,0:T(8,128)(2,1)} %get-tuple-element.44.low), custom_call_target="tpu_custom_call" | custom-call | tf_op jit(solution)/shard_map/hop/pallas_call | solution.py:52
  74.6 0.7 collective-permute-start.8
  75.9 2.3 %hop.17 = (f32[32,512]{1,0:T(8,128)}, f32[32,512]{1,0:T(8,128)}) custom-call(f32[32,512]{1,0:T(8,128)} %get-tuple-element.53.held, f32[32,512]{1,0:T(8,128)} %copy-done.11, f32[32,512]{1,0:T(8,128)} %get-tuple-element.42.base, bf16[512,512]{1,0:T(8,128)(2,1)} %get-tuple-element.43.high, bf16[512,512]{1,0:T(8,128)(2,1)} %get-tuple-element.44.low), custom_call_target="tpu_custom_call" | custom-call | tf_op jit(solution)/shard_map/hop/pallas_call | solution.py:52
  78.3 0.7 collective-permute-start.9
  79.6 5.5 %turn.1 = (f32[4,32,512]{2,1,0:T(8,128)}, f32[32,512]{1,0:T(8,128)}) custom-call(f32[32,512]{1,0:T(8,128)} %get-tuple-element.55.held, f32[32,512]{1,0:T(8,128)} %copy-done.9, f32[4,32,512]{2,1,0:T(8,128)} %get-tuple-element.57.cols, bf16[4,512,512]{2,1,0:T(8,128)(2,1)} %get-tuple-element.58.mh, bf16[4,512,512]{2,1,0:T(8,128)(2,1)} %get-tuple-element.59.ml), custom_call_target="tpu_custom_call" | custom-call | tf_op jit(solution)/shard_map/turn/pallas_call | solution.py:52
  86.4 2.3 %hop.18 = (f32[32,512]{1,0:T(8,128)}, f32[32,512]{1,0:T(8,128)}) custom-call(f32[32,512]{1,0:T(8,128)} %broadcast_in_dim.3.held, f32[32,512]{1,0:T(8,128)} %copy-done.22, f32[32,512]{1,0:T(8,128)} %get-tuple-element.60.base, bf16[512,512]{1,0:T(8,128)(2,1)} %get-tuple-element.61.high, bf16[512,512]{1,0:T(8,128)(2,1)} %get-tuple-element.62.low), custom_call_target="tpu_custom_call" | custom-call | tf_op jit(solution)/shard_map/hop/pallas_call | solution.py:52
  90.0 2.3 %hop.19 = (f32[32,512]{1,0:T(8,128)}, f32[32,512]{1,0:T(8,128)}) custom-call(f32[32,512]{1,0:T(8,128)} %get-tuple-element.63.held, f32[32,512]{1,0:T(8,128)} %copy-done.17, f32[32,512]{1,0:T(8,128)} %get-tuple-element.60.base, bf16[512,512]{1,0:T(8,128)(2,1)} %get-tuple-element.61.high, bf16[512,512]{1,0:T(8,128)(2,1)} %get-tuple-element.62.low), custom_call_target="tpu_custom_call" | custom-call | tf_op jit(solution)/shard_map/hop/pallas_call | solution.py:52
  93.6 2.3 %hop.20 = (f32[32,512]{1,0:T(8,128)}, f32[32,512]{1,0:T(8,128)}) custom-call(f32[32,512]{1,0:T(8,128)} %get-tuple-element.65.held, f32[32,512]{1,0:T(8,128)} %copy-done.18, f32[32,512]{1,0:T(8,128)} %get-tuple-element.60.base, bf16[512,512]{1,0:T(8,128)(2,1)} %get-tuple-element.61.high, bf16[512,512]{1,0:T(8,128)(2,1)} %get-tuple-element.62.low), custom_call_target="tpu_custom_call" | custom-call | tf_op jit(solution)/shard_map/hop/pallas_call | solution.py:52
  97.3 2.3 %hop.21 = (f32[32,512]{1,0:T(8,128)}, f32[32,512]{1,0:T(8,128)}) custom-call(f32[32,512]{1,0:T(8,128)} %get-tuple-element.67.held, f32[32,512]{1,0:T(8,128)} %copy-done.19, f32[32,512]{1,0:T(8,128)} %get-tuple-element.60.base, bf16[512,512]{1,0:T(8,128)(2,1)} %get-tuple-element.61.high, bf16[512,512]{1,0:T(8,128)(2,1)} %get-tuple-element.62.low), custom_call_target="tpu_custom_call" | custom-call | tf_op jit(solution)/shard_map/hop/pallas_call | solution.py:52
  100.9 2.3 %hop.22 = (f32[32,512]{1,0:T(8,128)}, f32[32,512]{1,0:T(8,128)}) custom-call(f32[32,512]{1,0:T(8,128)} %get-tuple-element.69.held, f32[32,512]{1,0:T(8,128)} %copy-done.20, f32[32,512]{1,0:T(8,128)} %get-tuple-element.60.base, bf16[512,512]{1,0:T(8,128)(2,1)} %get-tuple-element.61.high, bf16[512,512]{1,0:T(8,128)(2,1)} %get-tuple-element.62.low), custom_call_target="tpu_custom_call" | custom-call | tf_op jit(solution)/shard_map/hop/pallas_call | solution.py:52
  104.5 2.3 %hop.23 = (f32[32,512]{1,0:T(8,128)}, f32[32,512]{1,0:T(8,128)}) custom-call(f32[32,512]{1,0:T(8,128)} %get-tuple-element.71.held, f32[32,512]{1,0:T(8,128)} %copy-done.12, f32[32,512]{1,0:T(8,128)} %get-tuple-element.60.base, bf16[512,512]{1,0:T(8,128)(2,1)} %get-tuple-element.61.high, bf16[512,512]{1,0:T(8,128)(2,1)} %get-tuple-element.62.low), custom_call_target="tpu_custom_call" | custom-call | tf_op jit(solution)/shard_map/hop/pallas_call | solution.py:52
  106.9 1.3 collective-permute-start.16
  108.2 56.5 %collective-permute-done.16.came = f32[32,512]{1,0:T(8,128)S(1)} collective-permute-done((f32[32,512]{1,0:T(8,128)}, f32[32,512]{1,0:T(8,128)S(1)}, u32[]{:S(2)}, u32[]{:S(2)}) %collective-permute-start.16) | collective-permute-done | bytes 65568 | tf_op jit(solution)/shard_map/ppermute | solution.py:265
  165.2 4.6 %rise.1 = (f32[4,32,512]{2,1,0:T(8,128)}, f32[32,512]{1,0:T(8,128)}) custom-call(f32[32,512]{1,0:T(8,128)} %get-tuple-element.73.held, f32[32,512]{1,0:T(8,128)} %copy-done.8, f32[4,32,512]{2,1,0:T(8,128)} %get-tuple-element.75.lower, bf16[4,512,512]{2,1,0:T(8,128)(2,1)} %get-tuple-element.58.mh, bf16[4,512,512]{2,1,0:T(8,128)(2,1)} %get-tuple-element.59.ml), custom_call_target="tpu_custom_call" | custom-call | tf_op jit(solution)/shard_map/rise/pallas_call | solution.py:52
  169.8 0.9 slice.18
  170.8 0.8 slice.19
  171.6 1.7 collective-permute-start.17
  173.3 1.3 collective-permute-start.18
  174.6 4.6 %collective-permute-start.19 = (f32[2,1,128,128]{3,2,1,0:T(8,128)S(1)}, f32[2,1,128,128]{3,2,1,0:T(8,128)S(1)}, u32[]{:S(2)}, u32[]{:S(2)}) collective-permute-start(f32[2,1,128,128]{3,2,1,0:T(8,128)S(1)} %get-tuple-element.84), channel_id=1, source_target_pairs={{0,4},{4,8},{8,12},{12,16},{16,20},{20,24},{24,28},{1,5},{5,9},{9,... | collective-permute-start | bytes 393224 | tf_op jit(solution)/shard_map/ppermute | solution.py:234
  179.2 1.3 collective-permute-start.20
  181.2 2.0 pack.1
  183.2 3.5 %all-to-all-start.1 = ((f32[4,144,256]{2,1,0:T(8,128)}), f32[4,144,256]{2,1,0:T(8,128)S(1)}, u32[]{:S(2)}, u32[]{:S(2)}) async-start(f32[4,144,256]{2,1,0:T(8,128)} %pack.1), calls=%async_computation.1 | async-start | bytes 1179648 | tf_op jit(solution)/shard_map/all_to_all | solution.py:284
  186.8 2.3 %collective-permute-start.21 = (f32[2,6,8,128]{3,2,1,0:T(8,128)S(1)}, f32[2,6,8,128]{3,2,1,0:T(8,128)S(1)}, u32[]{:S(2)}, u32[]{:S(2)}) collective-permute-start(f32[2,6,8,128]{3,2,1,0:T(8,128)S(1)} %get-tuple-element.82), channel_id=1, source_target_pairs={{0,1},{1,2},{2,3},{4,5},{5,6},{6,7},{8,9},{9,10},{10,11},{12,13},{... | collective-permute-start | bytes 147464 | tf_op jit(solution)/shard_map/ppermute | solution.py:238
  189.1 1.3 collective-permute-start.22
  191.0 2.4 %collective-permute-done.22 = f32[2,6,8,128]{3,2,1,0:T(8,128)S(1)} collective-permute-done((f32[2,6,8,128]{3,2,1,0:T(8,128)S(1)}, f32[2,6,8,128]{3,2,1,0:T(8,128)S(1)}, u32[]{:S(2)}, u32[]{:S(2)}) %collective-permute-start.22) | collective-permute-done | bytes 49184 | tf_op jit(solution)/shard_map/ppermute | solution.py:239
  193.4 1.0 pad_maximum_fusion.extended
  194.4 2.1 apply_rhs.1.applied_rhs
  196.5 0.8 copy-done.2
  197.3 3.1 %images.1 = (f32[4,128,128]{2,1,0:T(8,128)}, f32[4,128,128]{2,1,0:T(8,128)}, f32[4,128,128]{2,1,0:T(8,128)}, f32[32,128]{1,0:T(8,128)}) custom-call(s32[4]{0:T(128)} %pad_add_fusion.where, f32[4,144,256]{2,1,0:T(8,128)} %copy-done.2, f32[2,6,144,128]{3,2,1,0:T(8,128)} %pad_maximum_fusion.extended, f32[4,128,128]{2,1,0:T(8,128)} %apply_rhs.1.applied_rhs), custom_call_target="tpu_custom_call" | custom-call | tf_op jit(solution)/shard_map/images/pallas_call | solution.py:52
  200.4 13.7 %all_to_all.21 = f32[32,1,128]{2,1,0:T(1,128)} all-to-all(f32[32,1,128]{2,1,0:T(1,128)} %bitcast.27), channel_id=1, replica_groups=mesh['layer'=8,'split'=4] {'layer','split'}, dimensions={0} | all-to-all | bytes 32768 | tf_op jit(solution)/shard_map/all_to_all | solution.py:294
  214.2 2.2 %finish.1 = (f32[4,128,128]{2,1,0:T(8,128)}, f32[4,128,128]{2,1,0:T(8,128)}) custom-call(f32[32,128]{1,0:T(8,128)} %bitcast.26, f32[4,128,128]{2,1,0:T(8,128)} %get-tuple-element.79.direction, f32[4,128,128]{2,1,0:T(8,128)} %get-tuple-element.80.image, f32[4,128,128]{2,1,0:T(8,128)} %get-tuple-element.81.applied_image, f32[4,128,128]{2,1,0:T(8,128)} %right_side.1, ...), custom_call_target="tpu_custom_call" | custom-call | tf_op jit(solution)/shard_map/finish/pallas_call | solution.py:52
  (78 shorter events, 16.3 us)
Async XLA Ops:
  0.6 26.4 %collective-permute-start = (f32[4,512,128]{2,1,0:T(8,128)}, f32[4,512,128]{2,1,0:T(8,128)S(1)}, u32[]{:S(2)}, u32[]{:S(2)}) collective-permute-start(f32[4,512,128]{2,1,0:T(8,128)} %refs_0_.1), channel_id=1, source_target_pairs={{0,2},{1,3},{2,0},{3,1},{4,6},{5,7},{6,4},{7,5},{8,10},{9,11},{10,... | collective-permute-start | bytes 3145736 | tf_op jit(solution)/shard_map/ppermute | solution.py:222
  3.7 34.7 %collective-permute-start.1 = (f32[4,512,128]{2,1,0:T(8,128)}, f32[4,512,128]{2,1,0:T(8,128)S(1)}, u32[]{:S(2)}, u32[]{:S(2)}) collective-permute-start(f32[4,512,128]{2,1,0:T(8,128)} %refs_0_.1), channel_id=1, source_target_pairs={{0,1},{1,0},{2,3},{3,2},{4,5},{5,4},{6,7},{7,6},{8,9},{9,8},{10,11... | collective-permute-start | bytes 3145736 | tf_op jit(solution)/shard_map/ppermute | solution.py:222
  27.1 11.4 %copy-start.3 = (f32[4,512,128]{2,1,0:T(8,128)}, f32[4,512,128]{2,1,0:T(8,128)S(1)}, u32[]{:S(2)}) copy-start(f32[4,512,128]{2,1,0:T(8,128)S(1)} %collective-permute-done.refs_1_) | copy-start | bytes 3145732
  27.1 11.4 %collective-permute-start.2 = (f32[4,512,128]{2,1,0:T(8,128)S(1)}, f32[4,512,128]{2,1,0:T(8,128)S(1)}, u32[]{:S(2)}, u32[]{:S(2)}) collective-permute-start(f32[4,512,128]{2,1,0:T(8,128)S(1)} %collective-permute-done.refs_1_), channel_id=1, source_target_pairs={{0,1},{1,0},{2,3},{3,2},{4,5},{5,4},{6,7},{7,6},{8,9},{9,8},{10,11... | collective-permute-start | bytes 3145736 | tf_op jit(solution)/shard_map/ppermute | solution.py:222
  29.0 9.4 %all-to-all-start = ((f32[4,4,32,128]{3,2,1,0:T(8,128)}), f32[4,4,32,128]{3,2,1,0:T(8,128)S(1)}, u32[]{:S(2)}, u32[]{:S(2)}) async-start(f32[4,4,32,128]{3,2,1,0:T(8,128)} %bitcast.24), calls=%async_computation | async-start | bytes 524288 | tf_op jit(solution)/shard_map/all_to_all | solution.py:228
  38.4 0.7 copy-start.6
  38.4 1.1 copy-start.4
  39.5 1.0 copy-start.5
  51.3 5.8 %collective-permute-start.3 = (f32[32,512]{1,0:T(8,128)}, f32[32,512]{1,0:T(8,128)S(1)}, u32[]{:S(2)}, u32[]{:S(2)}) collective-permute-start(f32[32,512]{1,0:T(8,128)} %get-tuple-element.42.base), channel_id=1, source_target_pairs={{0,4},{1,5},{2,6},{3,7}} | collective-permute-start | bytes 196616 | tf_op jit(solution)/shard_map/ppermute | solution.py:258
  57.2 0.6 copy-start.21
  60.1 0.7 collective-permute-start.4
  60.8 0.6 copy-start.13
  63.7 0.7 collective-permute-start.5
  64.4 0.6 copy-start.14
  67.4 0.7 collective-permute-start.6
  68.0 0.6 copy-start.15
  71.0 0.7 collective-permute-start.7
  71.7 0.6 copy-start.16
  74.6 0.7 collective-permute-start.8
  75.3 0.6 copy-start.11
  78.3 0.7 collective-permute-start.9
  78.9 0.6 copy-start.9
  85.1 0.7 collective-permute-start.10
  85.7 0.6 copy-start.22
  88.7 0.7 collective-permute-start.11
  89.4 0.6 copy-start.17
  92.3 0.7 collective-permute-start.12
  93.0 0.6 copy-start.18
  96.0 0.7 collective-permute-start.13
  96.6 0.6 copy-start.19
  99.6 0.7 collective-permute-start.14
  100.3 0.6 copy-start.20
  103.2 0.7 collective-permute-start.15
  103.9 0.6 copy-start.12
  106.9 57.7 %collective-permute-start.16 = (f32[32,512]{1,0:T(8,128)}, f32[32,512]{1,0:T(8,128)S(1)}, u32[]{:S(2)}, u32[]{:S(2)}) collective-permute-start(f32[32,512]{1,0:T(8,128)} %get-tuple-element.74), channel_id=1, source_target_pairs={{4,0},{5,1},{6,2},{7,3}} | collective-permute-start | bytes 196616 | tf_op jit(solution)/shard_map/ppermute | solution.py:265
  164.6 0.6 copy-start.8
  165.2 9.4 %copy-start = (f32[4,128,128]{2,1,0:T(8,128)S(1)}, f32[4,128,128]{2,1,0:T(8,128)}, u32[]{:S(2)}) copy-start(f32[4,128,128]{2,1,0:T(8,128)} %right_side.1) | copy-start | bytes 786436
  165.2 9.4 %copy-start.1 = (f32[4,128,128]{2,1,0:T(8,128)S(1)}, f32[4,128,128]{2,1,0:T(8,128)}, u32[]{:S(2)}) copy-start(f32[4,128,128]{2,1,0:T(8,128)} %param.4) | copy-start | bytes 786436
  171.6 8.9 %collective-permute-start.17 = (f32[2,32,512]{2,1,0:T(8,128)S(1)}, f32[2,32,512]{2,1,0:T(8,128)S(1)}, u32[]{:S(2)}, u32[]{:S(2)}) collective-permute-start(f32[2,32,512]{2,1,0:T(8,128)S(1)} %slice.18), channel_id=1, source_target_pairs={{0,4},{4,8},{8,12},{12,16},{16,20},{20,24},{24,28},{1,5},{5,9},{9,... | collective-permute-start | bytes 393224 | tf_op jit(solution)/shard_map/ppermute | solution.py:271
  173.3 7.2 %collective-permute-start.18 = (f32[1,32,512]{2,1,0:T(8,128)S(1)}, f32[1,32,512]{2,1,0:T(8,128)S(1)}, u32[]{:S(2)}, u32[]{:S(2)}) collective-permute-start(f32[1,32,512]{2,1,0:T(8,128)S(1)} %slice.19), channel_id=1, source_target_pairs={{4,0},{8,4},{12,8},{16,12},{20,16},{24,20},{28,24},{5,1},{9,5},{13... | collective-permute-start | bytes 196616 | tf_op jit(solution)/shard_map/ppermute | solution.py:272
  174.6 12.1 %collective-permute-start.19 = (f32[2,1,128,128]{3,2,1,0:T(8,128)S(1)}, f32[2,1,128,128]{3,2,1,0:T(8,128)S(1)}, u32[]{:S(2)}, u32[]{:S(2)}) collective-permute-start(f32[2,1,128,128]{3,2,1,0:T(8,128)S(1)} %get-tuple-element.84), channel_id=1, source_target_pairs={{0,4},{4,8},{8,12},{12,16},{16,20},{20,24},{24,28},{1,5},{5,9},{9,... | collective-permute-start | bytes 393224 | tf_op jit(solution)/shard_map/ppermute | solution.py:234
  179.2 7.5 %collective-permute-start.20 = (f32[2,1,128,128]{3,2,1,0:T(8,128)S(1)}, f32[2,1,128,128]{3,2,1,0:T(8,128)S(1)}, u32[]{:S(2)}, u32[]{:S(2)}) collective-permute-start(f32[2,1,128,128]{3,2,1,0:T(8,128)S(1)} %get-tuple-element.85), channel_id=1, source_target_pairs={{4,0},{8,4},{12,8},{16,12},{20,16},{24,20},{28,24},{5,1},{9,5},{13... | collective-permute-start | bytes 393224 | tf_op jit(solution)/shard_map/ppermute | solution.py:235
  180.5 0.6 copy-start.10
  180.5 0.7 copy-start.7
  183.2 13.2 %all-to-all-start.1 = ((f32[4,144,256]{2,1,0:T(8,128)}), f32[4,144,256]{2,1,0:T(8,128)S(1)}, u32[]{:S(2)}, u32[]{:S(2)}) async-start(f32[4,144,256]{2,1,0:T(8,128)} %pack.1), calls=%async_computation.1 | async-start | bytes 1179648 | tf_op jit(solution)/shard_map/all_to_all | solution.py:284
  186.8 4.3 %collective-permute-start.21 = (f32[2,6,8,128]{3,2,1,0:T(8,128)S(1)}, f32[2,6,8,128]{3,2,1,0:T(8,128)S(1)}, u32[]{:S(2)}, u32[]{:S(2)}) collective-permute-start(f32[2,6,8,128]{3,2,1,0:T(8,128)S(1)} %get-tuple-element.82), channel_id=1, source_target_pairs={{0,1},{1,2},{2,3},{4,5},{5,6},{6,7},{8,9},{9,10},{10,11},{12,13},{... | collective-permute-start | bytes 147464 | tf_op jit(solution)/shard_map/ppermute | solution.py:238
  189.1 4.3 %collective-permute-start.22 = (f32[2,6,8,128]{3,2,1,0:T(8,128)S(1)}, f32[2,6,8,128]{3,2,1,0:T(8,128)S(1)}, u32[]{:S(2)}, u32[]{:S(2)}) collective-permute-start(f32[2,6,8,128]{3,2,1,0:T(8,128)S(1)} %get-tuple-element.83), channel_id=1, source_target_pairs={{1,0},{2,1},{3,2},{5,4},{6,5},{7,6},{9,8},{10,9},{11,10},{13,12},{... | collective-permute-start | bytes 147464 | tf_op jit(solution)/shard_map/ppermute | solution.py:239
  196.5 0.8 copy-start.2

commit v2 on v1

--- a/solution.py
+++ b/solution.py
@@ -45,12 +45,23 @@
     return pairs[0]
 
 
-def call(body, out, *args, smem=0):
+def near(x):
+    return pltpu.with_memory_space_constraint(x, pltpu.VMEM)
+
+
+def call(body, out, *args, smem=0, stay=True, scratch=()):
     vm = pl.BlockSpec(memory_space=pltpu.VMEM)
     specs = [pl.BlockSpec(memory_space=pltpu.SMEM)] * smem + [vm] * (len(args) - smem)
-    shapes = [jax.ShapeDtypeStruct(s, d) for s, d in out]
+    shapes = [pltpu.VMEM(s, d) if stay else jax.ShapeDtypeStruct(s, d) for s, d in out]
+    args = args[:smem] + tuple(near(x) for x in args[smem:])
     return pl.pallas_call(
-        body, out_shape=shapes, in_specs=specs, out_specs=[vm] * len(shapes), name=body.__name__
+        body,
+        out_shape=shapes,
+        in_specs=specs,
+        out_specs=[vm] * len(shapes),
+        scratch_shapes=scratch,
+        name=body.__name__,
+        compiler_params=pltpu.CompilerParams(vmem_limit_bytes=32 * 1024 * 1024),
     )(*args)
 
 
@@ -214,16 +225,6 @@
     nx = inverses.shape[1]
     part = ny // splits
 
-    blocks = [inverses]
-    offsets = [0]
-    step = splits // 2
-    while step:
-        route = [(i, i ^ step) for i in range(splits)]
-        blocks = blocks + [lax.ppermute(b, "split", route) for b in blocks]
-        offsets = offsets + [o ^ step for o in offsets]
-        step //= 2
-    place = jnp.stack([own ^ o for o in offsets]).astype(jnp.int32)
-
     turned = jnp.swapaxes(right_side, 1, 2).reshape(planes, splits, part, width)
     pieces = lax.all_to_all(
         jnp.swapaxes(turned, 0, 1), "split", split_axis=0, concat_axis=0, tiled=True
@@ -240,6 +241,20 @@
     pair = jnp.concatenate([before, pair, after], axis=2)
     (applied_rhs,) = call(apply_rhs, [(right_side.shape, F32)], pair)
 
+    blocks = [inverses]
+    offsets = [0]
+    step = splits // 2
+    while step:
+        route = [(i, i ^ step) for i in range(splits)]
+        blocks = blocks + [lax.ppermute(b, "split", route) for b in blocks]
+        if len(blocks) == 2:
+            blocks[1], pieces, pair, applied_rhs = lax.optimization_barrier(
+                (blocks[1], pieces, pair, applied_rhs)
+            )
+        offsets = offsets + [o ^ step for o in offsets]
+        step //= 2
+    place = jnp.stack([own ^ o for o in offsets]).astype(jnp.int32)
+
     column = (part, nx)
     square = (nx, nx)
     stack = (planes,) + column
@@ -272,15 +287,15 @@
     ahead = lax.ppermute(swept[1:2], "layer", down)
     rows = width + 2 * EDGE
     packed = (planes + 4) * part
-    vm = pl.BlockSpec(memory_space=pltpu.VMEM)
-    windows = pl.pallas_call(
+    (windows,) = call(
         pack,
-        out_shape=jax.ShapeDtypeStruct((splits, rows, packed), F32),
-        in_specs=[vm] * 4,
-        out_specs=vm,
-        scratch_shapes=[pltpu.VMEM((nx + 2 * EDGE, packed), F32)],
-        name="pack",
-    )(swept, behind, above, ahead)
+        [((splits, rows, packed), F32)],
+        swept,
+        behind,
+        above,
+        ahead,
+        scratch=[pltpu.VMEM((nx + 2 * EDGE, packed), F32)],
+    )
     recv = lax.all_to_all(windows, "split", split_axis=0, concat_axis=0, tiled=True)
 
     where = jnp.stack(
@@ -294,7 +309,15 @@
     every = lax.all_to_all(sums, ("layer", "split"), split_axis=0, concat_axis=0, tiled=True)
     return tuple(
         call(
-            finish, [block] * 2, every, direction, image, applied_image, right_side, applied_rhs
+            finish,
+            [block] * 2,
+            every,
+            direction,
+            image,
+            applied_image,
+            right_side,
+            applied_rhs,
+            stay=False,
         )
     )
 

time: 217 us -> 155 us (0.71)
  Pallas kernels: 58.3 us -> 22.3 us
  local copies, waits for them, and re-layouts: 16 us -> 1.85 us
  waiting for transfers between devices: 89.8 us -> 81.9 us
  blocking collectives: 13.7 us -> 8.87 us
    pallas_call x18 -> x19, Pallas kernels: 56.3 us -> 22.3 us  [call(): pl.pallas_call(body, out_shape=shapes, in_specs=specs, out_specs=[vm] * l...]
    ppermute x3, waiting for transfers between devices: 23.4 us -> 2.55 us  [per_device(): blocks = blocks + [lax.ppermute(b, 'split', route) for b in blocks]]
    unnamed x47 -> x7, local copies, waits for them, and re-layouts: 12.9 us -> 1.09 us
    all_to_all x1, waiting for transfers between devices: 0.01 us -> 9.39 us  [per_device(): lax.all_to_all(windows, 'split', split_axis=0, concat_axis=0, tiled=True)]
    all_to_all x1, blocking collectives: 13.7 us -> 8.87 us  [per_device(): lax.all_to_all(sums, ('layer', 'split'), split_axis=0, concat_axis=0, til...]
    ppermute x1, waiting for transfers between devices: 0.01 us -> 4.86 us  [per_device(): ahead = lax.ppermute(swept[1:2], 'layer', down)]
    ppermute x3, starting transfers between devices: 3.07 us -> 6.09 us  [per_device(): blocks = blocks + [lax.ppermute(b, 'split', route) for b in blocks]]
    all_to_all x1, waiting for transfers between devices: 5.37 us -> 8.33 us  [per_device(): lax.all_to_all(jnp.swapaxes(turned, 0, 1), 'split', split_axis=0, concat_...]
  transfers between devices with their start and end apart: 25 -> 25, of which waited for: 5 -> 8; matrix products, arithmetic and copies ran while one was open for 2% -> 2% of each run, Pallas kernels for 2% -> 0%
where the time goes in v2:
time: 155 us; the launch traced here: 154 us
  waiting for transfers between devices  81.9 us (53%)
  starting transfers between devices  36.9 us (24%)
  Pallas kernels  22.3 us (14%)
  blocking collectives  8.87 us (6%)
  local copies, waits for them, and re-layouts  1.85 us (1%)
    ppermute x7, waiting for transfers between devices, per_device(): came = lax.ppermute(out, 'layer', [(depth - 1 - t, depth - 2 - t)])  53.9 us
    pallas_call x19, Pallas kernels, call(): pl.pallas_call(body, out_shape=shapes, in_specs=specs, out_specs=[vm] * l...  22.3 us
    all_to_all x1, waiting for transfers between devices, per_device(): lax.all_to_all(windows, 'split', split_axis=0, concat_axis=0, tiled=True)  9.39 us
    all_to_all x1, blocking collectives, per_device(): lax.all_to_all(sums, ('layer', 'split'), split_axis=0, concat_axis=0, til...  8.87 us
    all_to_all x1, waiting for transfers between devices, per_device(): lax.all_to_all(jnp.swapaxes(turned, 0, 1), 'split', split_axis=0, concat_...  8.33 us
    ppermute x7, starting transfers between devices, per_device(): came = lax.ppermute(out, 'layer', [(t, t + 1)])  7.67 us
    ppermute x3, starting transfers between devices, per_device(): blocks = blocks + [lax.ppermute(b, 'split', route) for b in blocks]  6.09 us
    ppermute x7, starting transfers between devices, per_device(): came = lax.ppermute(out, 'layer', [(depth - 1 - t, depth - 2 - t)])  5.35 us
  transfers between devices with their start and end apart: 25, of which 8 were waited for; matrix products, arithmetic and copies ran while one was open for 2% of the time, Pallas kernels for 0%

profile of v2, /device:TPU:0, one launch (start us, length us, event | category | flops | bytes accessed | tf_op | source)
XLA Modules:
  0.0 154.0 jit_solution(5710237039817101347)
XLA Ops:
  0.7 3.1 %collective-permute-start = (f32[4,512,128]{2,1,0:T(8,128)}, f32[4,512,128]{2,1,0:T(8,128)}, u32[]{:S(2)}, u32[]{:S(2)}) collective-permute-start(f32[4,512,128]{2,1,0:T(8,128)} %refs_0_.1), channel_id=1, source_target_pairs={{0,2},{1,3},{2,0},{3,1},{4,6},{5,7},{6,4},{7,5},{8,10},{9,11},{10,... | collective-permute-start | bytes 3145736 | tf_op jit(solution)/shard_map/ppermute | solution.py:249
  3.7 1.0 pad_maximum_fusion.2
  4.7 3.4 %collective-permute-start.1 = (f32[2,1,128,128]{3,2,1,0:T(8,128)S(1)}, f32[2,1,128,128]{3,2,1,0:T(8,128)S(1)}, u32[]{:S(2)}, u32[]{:S(2)}) collective-permute-start(f32[2,1,128,128]{3,2,1,0:T(8,128)S(1)} %get-tuple-element.92), channel_id=1, source_target_pairs={{0,4},{4,8},{8,12},{12,16},{16,20},{20,24},{24,28},{1,5},{5,9},{9,... | collective-permute-start | bytes 393224 | tf_op jit(solution)/shard_map/ppermute | solution.py:235
  8.1 1.3 collective-permute-start.2
  9.4 1.1 copy.7
  10.5 0.7 copy.11
  11.2 3.4 %all-to-all-start = ((f32[4,4,32,128]{3,2,1,0:T(8,128)}), f32[4,4,32,128]{3,2,1,0:T(8,128)S(1)}, u32[]{:S(2)}, u32[]{:S(2)}) async-start(f32[4,4,32,128]{3,2,1,0:T(8,128)} %bitcast.17), calls=%async_computation | async-start | bytes 524288 | tf_op jit(solution)/shard_map/all_to_all | solution.py:229
  15.0 2.1 %collective-permute-start.3 = (f32[2,6,8,128]{3,2,1,0:T(8,128)S(1)}, f32[2,6,8,128]{3,2,1,0:T(8,128)S(1)}, u32[]{:S(2)}, u32[]{:S(2)}) collective-permute-start(f32[2,6,8,128]{3,2,1,0:T(8,128)S(1)} %get-tuple-element.90), channel_id=1, source_target_pairs={{0,1},{1,2},{2,3},{4,5},{5,6},{6,7},{8,9},{9,10},{10,11},{12,13},{... | collective-permute-start | bytes 147464 | tf_op jit(solution)/shard_map/ppermute | solution.py:239
  17.0 1.3 collective-permute-start.4
  18.3 2.3 %collective-permute-start.5 = (f32[4,512,128]{2,1,0:T(8,128)S(1)}, f32[4,512,128]{2,1,0:T(8,128)}, u32[]{:S(2)}, u32[]{:S(2)}) collective-permute-start(f32[4,512,128]{2,1,0:T(8,128)S(1)} %copy-done.1), channel_id=1, source_target_pairs={{0,1},{1,0},{2,3},{3,2},{4,5},{5,4},{6,7},{7,6},{8,9},{9,8},{10,11... | collective-permute-start | bytes 3145736 | tf_op jit(solution)/shard_map/ppermute | solution.py:249
  20.7 0.6 collective-permute-done.4
  21.6 8.3 %all-to-all-done.refs_4_ = f32[4,4,32,128]{3,2,1,0:T(8,128)S(1)} async-done(((f32[4,4,32,128]{3,2,1,0:T(8,128)}), f32[4,4,32,128]{3,2,1,0:T(8,128)S(1)}, u32[]{:S(2)}, u32[]{:S(2)}) %all-to-all-start) | async-done | bytes 262176 | tf_op jit(solution)/shard_map/all_to_all | solution.py:229
  29.9 0.7 collective-permute-start.6
  30.7 2.5 %collective-permute-done.6.refs_3_ = f32[4,512,128]{2,1,0:T(8,128)} collective-permute-done((f32[4,512,128]{2,1,0:T(8,128)}, f32[4,512,128]{2,1,0:T(8,128)}, u32[]{:S(2)}, u32[]{:S(2)}) %collective-permute-start.6) | collective-permute-done | bytes 1048608 | tf_op jit(solution)/shard_map/ppermute | solution.py:249
  33.2 9.5 %prepare.1 = (bf16[4,512,512]{2,1,0:T(8,128)(2,1)S(1)}, bf16[4,512,512]{2,1,0:T(8,128)(2,1)S(1)}, bf16[512,512]{1,0:T(8,128)(2,1)S(1)}, bf16[512,512]{1,0:T(8,12...) custom-call(s32[4]{0:T(128)S(1)} %pad_add_fusion.1.place, ...), custom_call_target="tpu_custom_call" | custom-call | tf_op jit(solution)/shard_map/prepare/pallas_call | solution.py:57
  42.7 3.6 %collective-permute-start.7 = (f32[32,512]{1,0:T(8,128)S(1)}, f32[32,512]{1,0:T(8,128)S(1)}, u32[]{:S(2)}, u32[]{:S(2)}) collective-permute-start(f32[32,512]{1,0:T(8,128)S(1)} %get-tuple-element.48.base), channel_id=1, source_target_pairs={{0,4},{1,5},{2,6},{3,7}} | collective-permute-start | bytes 196616 | tf_op jit(solution)/shard_map/ppermute | solution.py:273
  46.4 1.9 %collective-permute-done.7.came = f32[32,512]{1,0:T(8,128)S(1)} collective-permute-done((f32[32,512]{1,0:T(8,128)S(1)}, f32[32,512]{1,0:T(8,128)S(1)}, u32[]{:S(2)}, u32[]{:S(2)}) %collective-permute-start.7) | collective-permute-done | bytes 65568 | tf_op jit(solution)/shard_map/ppermute | solution.py:273
  48.6 0.7 collective-permute-start.8
  49.7 0.7 collective-permute-start.9
  50.4 0.4 hop.14
  50.8 0.7 collective-permute-start.10
  51.5 0.4 hop.15
  51.9 0.7 collective-permute-start.11
  52.6 0.4 hop.16
  53.1 0.7 collective-permute-start.12
  54.2 0.7 collective-permute-start.13
  54.8 2.5 %turn.1 = (f32[4,32,512]{2,1,0:T(8,128)S(1)}, f32[32,512]{1,0:T(8,128)S(1)}) custom-call(f32[32,512]{1,0:T(8,128)S(1)} %get-tuple-element.61.held, f32[32,512]{1,0:T(8,128)S(1)} %collective-permute-done.13.came, f32[4,32,512]{2,1,0:T(8,128)S(1)} %get-tuple-element.63.cols, bf16[4,512,512]{2,1,0:T(8,128)(2,1)S(1)} %get-tuple-element.64.mh, ...), custom_call_target="tpu_custom_call" | custom-call | tf_op jit(solution)/shard_map/turn/pallas_call | solution.py:57
  57.4 0.7 collective-permute-start.14
  58.1 0.4 hop.18
  58.5 0.7 collective-permute-start.15
  59.2 0.4 hop.19
  59.6 0.7 collective-permute-start.16
  60.7 0.7 collective-permute-start.17
  61.8 0.7 collective-permute-start.18
  62.5 0.4 hop.22
  62.9 0.7 collective-permute-start.19
  64.0 1.3 collective-permute-start.20
  65.3 53.9 %collective-permute-done.20.came = f32[32,512]{1,0:T(8,128)S(1)} collective-permute-done((f32[32,512]{1,0:T(8,128)S(1)}, f32[32,512]{1,0:T(8,128)S(1)}, u32[]{:S(2)}, u32[]{:S(2)}) %collective-permute-start.20) | collective-permute-done | bytes 65568 | tf_op jit(solution)/shard_map/ppermute | solution.py:280
  119.2 1.5 rise.1
  120.7 1.6 %collective-permute-start.21 = (f32[2,32,512]{2,1,0:T(8,128)S(1)}, f32[2,32,512]{2,1,0:T(8,128)S(1)}, u32[]{:S(2)}, u32[]{:S(2)}) collective-permute-start(f32[2,32,512]{2,1,0:T(8,128)S(1)} %slice.22), channel_id=1, source_target_pairs={{0,4},{4,8},{8,12},{12,16},{16,20},{20,24},{24,28},{1,5},{5,9},{9,... | collective-permute-start | bytes 393224 | tf_op jit(solution)/shard_map/ppermute | solution.py:286
  122.3 1.3 collective-permute-start.22
  123.6 4.9 %collective-permute-done.22.ahead = f32[1,32,512]{2,1,0:T(8,128)S(1)} collective-permute-done((f32[1,32,512]{2,1,0:T(8,128)S(1)}, f32[1,32,512]{2,1,0:T(8,128)S(1)}, u32[]{:S(2)}, u32[]{:S(2)}) %collective-permute-start.22) | collective-permute-done | bytes 65568 | tf_op jit(solution)/shard_map/ppermute | solution.py:287
  128.5 1.0 pack.1
  129.5 3.5 %all-to-all-start.1 = ((f32[4,144,256]{2,1,0:T(8,128)}), f32[4,144,256]{2,1,0:T(8,128)S(1)}, u32[]{:S(2)}, u32[]{:S(2)}) async-start(f32[4,144,256]{2,1,0:T(8,128)} %pack.1), calls=%async_computation.1 | async-start | bytes 1179648 | tf_op jit(solution)/shard_map/all_to_all | solution.py:299
  133.1 9.4 %all-to-all-done.1.recv = f32[4,144,256]{2,1,0:T(8,128)S(1)} async-done(((f32[4,144,256]{2,1,0:T(8,128)}), f32[4,144,256]{2,1,0:T(8,128)S(1)}, u32[]{:S(2)}, u32[]{:S(2)}) %all-to-all-start.1) | async-done | bytes 589856 | tf_op jit(solution)/shard_map/all_to_all | solution.py:299
  142.5 1.7 %images.1 = (f32[4,128,128]{2,1,0:T(8,128)S(1)}, f32[4,128,128]{2,1,0:T(8,128)S(1)}, f32[4,128,128]{2,1,0:T(8,128)S(1)}, f32[32,128]{1,0:T(8,128)S(1)}) custom-call(s32[4]{0:T(128)S(1)} %pad_add_fusion.where, f32[4,144,256]{2,1,0:T(8,128)S(1)} %all-to-all-done.1.recv, f32[2,6,144,128]{3,2,1,0:T(8,128)S(1)} %pad_maximum_fusion.extended, ...), custom_call_target="tpu_custom_call" | custom-call | tf_op jit(solution)/shard_map/images/pallas_call | solution.py:57
  144.2 8.9 %all_to_all.21 = f32[32,1,128]{2,1,0:T(1,128)S(1)} all-to-all(f32[32,1,128]{2,1,0:T(1,128)S(1)} %bitcast.22), channel_id=1, replica_groups=mesh['layer'=8,'split'=4] {'layer','split'}, dimensions={0} | all-to-all | bytes 32768 | tf_op jit(solution)/shard_map/all_to_all | solution.py:309
  153.0 1.0 finish.1
  (38 shorter events, 3.3 us)
Async XLA Ops:
  0.6 17.7 %copy-start.1 = (f32[4,512,128]{2,1,0:T(8,128)S(1)}, f32[4,512,128]{2,1,0:T(8,128)}, u32[]{:S(2)}) copy-start(f32[4,512,128]{2,1,0:T(8,128)} %refs_0_.1) | copy-start | bytes 3145732
  0.6 14.3 %copy-start.2 = (f32[4,128,128]{2,1,0:T(8,128)S(1)}, f32[4,128,128]{2,1,0:T(8,128)}, u32[]{:S(2)}) copy-start(f32[4,128,128]{2,1,0:T(8,128)} %param.4) | copy-start | bytes 786436
  0.6 14.3 %copy-start = (f32[4,128,128]{2,1,0:T(8,128)S(1)}, f32[4,128,128]{2,1,0:T(8,128)}, u32[]{:S(2)}) copy-start(f32[4,128,128]{2,1,0:T(8,128)} %right_side.1) | copy-start | bytes 786436
  0.7 29.2 %collective-permute-start = (f32[4,512,128]{2,1,0:T(8,128)}, f32[4,512,128]{2,1,0:T(8,128)}, u32[]{:S(2)}, u32[]{:S(2)}) collective-permute-start(f32[4,512,128]{2,1,0:T(8,128)} %refs_0_.1), channel_id=1, source_target_pairs={{0,2},{1,3},{2,0},{3,1},{4,6},{5,7},{6,4},{7,5},{8,10},{9,11},{10,... | collective-permute-start | bytes 3145736 | tf_op jit(solution)/shard_map/ppermute | solution.py:249
  4.7 9.9 %collective-permute-start.1 = (f32[2,1,128,128]{3,2,1,0:T(8,128)S(1)}, f32[2,1,128,128]{3,2,1,0:T(8,128)S(1)}, u32[]{:S(2)}, u32[]{:S(2)}) collective-permute-start(f32[2,1,128,128]{3,2,1,0:T(8,128)S(1)} %get-tuple-element.92), channel_id=1, source_target_pairs={{0,4},{4,8},{8,12},{12,16},{16,20},{20,24},{24,28},{1,5},{5,9},{9,... | collective-permute-start | bytes 393224 | tf_op jit(solution)/shard_map/ppermute | solution.py:235
  8.1 6.9 %collective-permute-start.2 = (f32[2,1,128,128]{3,2,1,0:T(8,128)S(1)}, f32[2,1,128,128]{3,2,1,0:T(8,128)S(1)}, u32[]{:S(2)}, u32[]{:S(2)}) collective-permute-start(f32[2,1,128,128]{3,2,1,0:T(8,128)S(1)} %get-tuple-element.93), channel_id=1, source_target_pairs={{4,0},{8,4},{12,8},{16,12},{20,16},{24,20},{28,24},{5,1},{9,5},{13... | collective-permute-start | bytes 393224 | tf_op jit(solution)/shard_map/ppermute | solution.py:236
  11.2 18.7 %all-to-all-start = ((f32[4,4,32,128]{3,2,1,0:T(8,128)}), f32[4,4,32,128]{3,2,1,0:T(8,128)S(1)}, u32[]{:S(2)}, u32[]{:S(2)}) async-start(f32[4,4,32,128]{3,2,1,0:T(8,128)} %bitcast.17), calls=%async_computation | async-start | bytes 524288 | tf_op jit(solution)/shard_map/all_to_all | solution.py:229
  15.0 5.7 %collective-permute-start.3 = (f32[2,6,8,128]{3,2,1,0:T(8,128)S(1)}, f32[2,6,8,128]{3,2,1,0:T(8,128)S(1)}, u32[]{:S(2)}, u32[]{:S(2)}) collective-permute-start(f32[2,6,8,128]{3,2,1,0:T(8,128)S(1)} %get-tuple-element.90), channel_id=1, source_target_pairs={{0,1},{1,2},{2,3},{4,5},{5,6},{6,7},{8,9},{9,10},{10,11},{12,13},{... | collective-permute-start | bytes 147464 | tf_op jit(solution)/shard_map/ppermute | solution.py:239
  17.0 4.3 %collective-permute-start.4 = (f32[2,6,8,128]{3,2,1,0:T(8,128)S(1)}, f32[2,6,8,128]{3,2,1,0:T(8,128)S(1)}, u32[]{:S(2)}, u32[]{:S(2)}) collective-permute-start(f32[2,6,8,128]{3,2,1,0:T(8,128)S(1)} %get-tuple-element.91), channel_id=1, source_target_pairs={{1,0},{2,1},{3,2},{5,4},{6,5},{7,6},{9,8},{10,9},{11,10},{13,12},{... | collective-permute-start | bytes 147464 | tf_op jit(solution)/shard_map/ppermute | solution.py:240
  18.3 12.3 %collective-permute-start.5 = (f32[4,512,128]{2,1,0:T(8,128)S(1)}, f32[4,512,128]{2,1,0:T(8,128)}, u32[]{:S(2)}, u32[]{:S(2)}) collective-permute-start(f32[4,512,128]{2,1,0:T(8,128)S(1)} %copy-done.1), channel_id=1, source_target_pairs={{0,1},{1,0},{2,3},{3,2},{4,5},{5,4},{6,7},{7,6},{8,9},{9,8},{10,11... | collective-permute-start | bytes 3145736 | tf_op jit(solution)/shard_map/ppermute | solution.py:249
  29.9 3.3 %collective-permute-start.6 = (f32[4,512,128]{2,1,0:T(8,128)}, f32[4,512,128]{2,1,0:T(8,128)}, u32[]{:S(2)}, u32[]{:S(2)}) collective-permute-start(f32[4,512,128]{2,1,0:T(8,128)} %collective-permute-done.refs_1_), channel_id=1, source_target_pairs={{0,1},{1,0},{2,3},{3,2},{4,5},{5,4},{6,7},{7,6},{8,9},{9,8},{10,11... | collective-permute-start | bytes 3145736 | tf_op jit(solution)/shard_map/ppermute | solution.py:249
  42.7 5.5 %collective-permute-start.7 = (f32[32,512]{1,0:T(8,128)S(1)}, f32[32,512]{1,0:T(8,128)S(1)}, u32[]{:S(2)}, u32[]{:S(2)}) collective-permute-start(f32[32,512]{1,0:T(8,128)S(1)} %get-tuple-element.48.base), channel_id=1, source_target_pairs={{0,4},{1,5},{2,6},{3,7}} | collective-permute-start | bytes 196616 | tf_op jit(solution)/shard_map/ppermute | solution.py:273
  48.6 0.7 collective-permute-start.8
  49.7 0.7 collective-permute-start.9
  50.8 0.7 collective-permute-start.10
  51.9 0.7 collective-permute-start.11
  53.1 0.7 collective-permute-start.12
  54.2 0.7 collective-permute-start.13
  57.4 0.7 collective-permute-start.14
  58.5 0.7 collective-permute-start.15
  59.6 0.7 collective-permute-start.16
  60.7 0.7 collective-permute-start.17
  61.8 0.7 collective-permute-start.18
  62.9 0.7 collective-permute-start.19
  64.0 55.2 %collective-permute-start.20 = (f32[32,512]{1,0:T(8,128)S(1)}, f32[32,512]{1,0:T(8,128)S(1)}, u32[]{:S(2)}, u32[]{:S(2)}) collective-permute-start(f32[32,512]{1,0:T(8,128)S(1)} %get-tuple-element.80), channel_id=1, source_target_pairs={{4,0},{5,1},{6,2},{7,3}} | collective-permute-start | bytes 196616 | tf_op jit(solution)/shard_map/ppermute | solution.py:280
  120.7 7.8 %collective-permute-start.21 = (f32[2,32,512]{2,1,0:T(8,128)S(1)}, f32[2,32,512]{2,1,0:T(8,128)S(1)}, u32[]{:S(2)}, u32[]{:S(2)}) collective-permute-start(f32[2,32,512]{2,1,0:T(8,128)S(1)} %slice.22), channel_id=1, source_target_pairs={{0,4},{4,8},{8,12},{12,16},{16,20},{20,24},{24,28},{1,5},{5,9},{9,... | collective-permute-start | bytes 393224 | tf_op jit(solution)/shard_map/ppermute | solution.py:286
  122.3 6.2 %collective-permute-start.22 = (f32[1,32,512]{2,1,0:T(8,128)S(1)}, f32[1,32,512]{2,1,0:T(8,128)S(1)}, u32[]{:S(2)}, u32[]{:S(2)}) collective-permute-start(f32[1,32,512]{2,1,0:T(8,128)S(1)} %slice.23), channel_id=1, source_target_pairs={{4,0},{8,4},{12,8},{16,12},{20,16},{24,20},{28,24},{5,1},{9,5},{13... | collective-permute-start | bytes 196616 | tf_op jit(solution)/shard_map/ppermute | solution.py:287
  129.5 13.0 %all-to-all-start.1 = ((f32[4,144,256]{2,1,0:T(8,128)}), f32[4,144,256]{2,1,0:T(8,128)S(1)}, u32[]{:S(2)}, u32[]{:S(2)}) async-start(f32[4,144,256]{2,1,0:T(8,128)} %pack.1), calls=%async_computation.1 | async-start | bytes 1179648 | tf_op jit(solution)/shard_map/all_to_all | solution.py:299

commit v3 on v2

--- a/solution.py
+++ b/solution.py
@@ -68,7 +68,7 @@
 def prepare(place, *refs):
     count = place.shape[0]
     blocks = refs[:count]
-    pieces, mh, ml, ph, plo, qh, qlo, tail, cols = refs[count:]
+    pieces, mh, ml, ph, plo, tail, cols = refs[count:]
     planes, nx, width = blocks[0].shape
     for j in range(count):
         at = pl.multiple_of(place[j] * width, width)
@@ -85,6 +85,10 @@
     tail[...] = state
     order = [(mh[k], ml[k]) for k in range(planes)]
     ph[...], plo[...] = chain_product(order[::-1])
+
+
+def prepare_up(mh, ml, qh, qlo):
+    order = [(mh[k], ml[k]) for k in range(mh.shape[0])]
     qh[...], qlo[...] = chain_product(order)
 
 
@@ -258,19 +262,23 @@
     column = (part, nx)
     square = (nx, nx)
     stack = (planes,) + column
-    mh, ml, ph, plo, qh, qlo, tail, cols = call(
+    mh, ml, ph, plo, tail, cols = call(
         prepare,
-        [((planes,) + square, BF16)] * 2 + [(square, BF16)] * 4 + [(column, F32), (stack, F32)],
+        [((planes,) + square, BF16)] * 2 + [(square, BF16)] * 2 + [(column, F32), (stack, F32)],
         place,
         *blocks,
         pieces,
         smem=1,
     )
 
+    qh, qlo = call(prepare_up, [(square, BF16)] * 2, mh, ml)
+
     zero = jnp.zeros(column, F32)
     held, out = zero, tail
     for t in range(depth - 1):
         came = lax.ppermute(out, "layer", [(t, t + 1)])
+        if t == 0:
+            came, qh, qlo = lax.optimization_barrier((came, qh, qlo))
         if t < depth - 2:
             held, out = call(hop, [(column, F32)] * 2, held, came, tail, ph, plo)
     lower, top = call(turn, [(stack, F32), (column, F32)], held, came, cols, mh, ml)

time: 155 us -> 152 us (0.981)
  waiting for transfers between devices: 81.9 us -> 79.2 us
    ppermute x7, waiting for transfers between devices: 1.9 us -> 0.02 us  [per_device(): came = lax.ppermute(out, 'layer', [(t, t + 1)])]
    pallas_call x19 -> x20, Pallas kernels: 22.3 us -> 22.4 us  [call(): pl.pallas_call(body, out_shape=shapes, in_specs=specs, out_specs=[vm] * l...]
  transfers between devices with their start and end apart: 25 -> 25, of which waited for: 8 -> 7; matrix products, arithmetic and copies ran while one was open for 2% -> 2% of each run, Pallas kernels for 0% -> 2%
where the time goes in v3:
time: 152 us; the launch traced here: 151 us
  waiting for transfers between devices  79.2 us (52%)
  starting transfers between devices  36.9 us (24%)
  Pallas kernels  22.4 us (15%)
  blocking collectives  8.87 us (6%)
  local copies, waits for them, and re-layouts  1.86 us (1%)
    ppermute x7, waiting for transfers between devices, per_device(): came = lax.ppermute(out, 'layer', [(depth - 1 - t, depth - 2 - t)])  53.1 us
    pallas_call x20, Pallas kernels, call(): pl.pallas_call(body, out_shape=shapes, in_specs=specs, out_specs=[vm] * l...  22.4 us
    all_to_all x1, waiting for transfers between devices, per_device(): lax.all_to_all(windows, 'split', split_axis=0, concat_axis=0, tiled=True)  9.39 us
    all_to_all x1, blocking collectives, per_device(): lax.all_to_all(sums, ('layer', 'split'), split_axis=0, concat_axis=0, til...  8.87 us
    all_to_all x1, waiting for transfers between devices, per_device(): lax.all_to_all(jnp.swapaxes(turned, 0, 1), 'split', split_axis=0, concat_...  8.33 us
    ppermute x7, starting transfers between devices, per_device(): came = lax.ppermute(out, 'layer', [(t, t + 1)])  7.67 us
    ppermute x3, starting transfers between devices, per_device(): blocks = blocks + [lax.ppermute(b, 'split', route) for b in blocks]  6.09 us
    ppermute x7, starting transfers between devices, per_device(): came = lax.ppermute(out, 'layer', [(depth - 1 - t, depth - 2 - t)])  5.35 us
  transfers between devices with their start and end apart: 25, of which 7 were waited for; matrix products, arithmetic and copies ran while one was open for 2% of the time, Pallas kernels for 2%

profile of v3, /device:TPU:0, one launch (start us, length us, event | category | flops | bytes accessed | tf_op | source)
XLA Modules:
  0.0 151.5 jit_solution(5371591478467485049)
XLA Ops:
  0.7 3.1 %collective-permute-start = (f32[4,512,128]{2,1,0:T(8,128)}, f32[4,512,128]{2,1,0:T(8,128)}, u32[]{:S(2)}, u32[]{:S(2)}) collective-permute-start(f32[4,512,128]{2,1,0:T(8,128)} %refs_0_.1), channel_id=1, source_target_pairs={{0,2},{1,3},{2,0},{3,1},{4,6},{5,7},{6,4},{7,5},{8,10},{9,11},{10,... | collective-permute-start | bytes 3145736 | tf_op jit(solution)/shard_map/ppermute | solution.py:253
  3.7 1.0 pad_maximum_fusion.2
  4.7 3.4 %collective-permute-start.1 = (f32[2,1,128,128]{3,2,1,0:T(8,128)S(1)}, f32[2,1,128,128]{3,2,1,0:T(8,128)S(1)}, u32[]{:S(2)}, u32[]{:S(2)}) collective-permute-start(f32[2,1,128,128]{3,2,1,0:T(8,128)S(1)} %get-tuple-element.98), channel_id=1, source_target_pairs={{0,4},{4,8},{8,12},{12,16},{16,20},{20,24},{24,28},{1,5},{5,9},{9,... | collective-permute-start | bytes 393224 | tf_op jit(solution)/shard_map/ppermute | solution.py:239
  8.1 1.3 collective-permute-start.2
  9.4 1.1 copy.7
  10.5 0.7 copy.11
  11.2 3.4 %all-to-all-start = ((f32[4,4,32,128]{3,2,1,0:T(8,128)}), f32[4,4,32,128]{3,2,1,0:T(8,128)S(1)}, u32[]{:S(2)}, u32[]{:S(2)}) async-start(f32[4,4,32,128]{3,2,1,0:T(8,128)} %bitcast.17), calls=%async_computation | async-start | bytes 524288 | tf_op jit(solution)/shard_map/all_to_all | solution.py:233
  15.0 2.1 %collective-permute-start.3 = (f32[2,6,8,128]{3,2,1,0:T(8,128)S(1)}, f32[2,6,8,128]{3,2,1,0:T(8,128)S(1)}, u32[]{:S(2)}, u32[]{:S(2)}) collective-permute-start(f32[2,6,8,128]{3,2,1,0:T(8,128)S(1)} %get-tuple-element.96), channel_id=1, source_target_pairs={{0,1},{1,2},{2,3},{4,5},{5,6},{6,7},{8,9},{9,10},{10,11},{12,13},{... | collective-permute-start | bytes 147464 | tf_op jit(solution)/shard_map/ppermute | solution.py:243
  17.0 1.3 collective-permute-start.4
  18.3 2.3 %collective-permute-start.5 = (f32[4,512,128]{2,1,0:T(8,128)S(1)}, f32[4,512,128]{2,1,0:T(8,128)}, u32[]{:S(2)}, u32[]{:S(2)}) collective-permute-start(f32[4,512,128]{2,1,0:T(8,128)S(1)} %copy-done.1), channel_id=1, source_target_pairs={{0,1},{1,0},{2,3},{3,2},{4,5},{5,4},{6,7},{7,6},{8,9},{9,8},{10,11... | collective-permute-start | bytes 3145736 | tf_op jit(solution)/shard_map/ppermute | solution.py:253
  20.7 0.6 collective-permute-done.4
  21.6 8.3 %all-to-all-done.refs_4_ = f32[4,4,32,128]{3,2,1,0:T(8,128)S(1)} async-done(((f32[4,4,32,128]{3,2,1,0:T(8,128)}), f32[4,4,32,128]{3,2,1,0:T(8,128)S(1)}, u32[]{:S(2)}, u32[]{:S(2)}) %all-to-all-start) | async-done | bytes 262176 | tf_op jit(solution)/shard_map/all_to_all | solution.py:233
  29.9 0.7 collective-permute-start.6
  30.7 2.5 %collective-permute-done.6.refs_3_ = f32[4,512,128]{2,1,0:T(8,128)} collective-permute-done((f32[4,512,128]{2,1,0:T(8,128)}, f32[4,512,128]{2,1,0:T(8,128)}, u32[]{:S(2)}, u32[]{:S(2)}) %collective-permute-start.6) | collective-permute-done | bytes 1048608 | tf_op jit(solution)/shard_map/ppermute | solution.py:253
  33.2 7.0 %prepare.1 = (bf16[4,512,512]{2,1,0:T(8,128)(2,1)S(1)}, bf16[4,512,512]{2,1,0:T(8,128)(2,1)S(1)}, bf16[512,512]{1,0:T(8,128)(2,1)S(1)}, bf16[512,512]{1,0:T(8,12...) custom-call(s32[4]{0:T(128)S(1)} %pad_add_fusion.1.place, f32[4,512,128]{2,1,0:T(8,128)S(1)} %copy-done.1, ...), custom_call_target="tpu_custom_call" | custom-call | tf_op jit(solution)/shard_map/prepare/pallas_call | solution.py:57
  40.2 3.6 %collective-permute-start.7 = (f32[32,512]{1,0:T(8,128)S(1)}, f32[32,512]{1,0:T(8,128)S(1)}, u32[]{:S(2)}, u32[]{:S(2)}) collective-permute-start(f32[32,512]{1,0:T(8,128)S(1)} %get-tuple-element.51.base), channel_id=1, source_target_pairs={{0,4},{1,5},{2,6},{3,7}} | collective-permute-start | bytes 196616 | tf_op jit(solution)/shard_map/ppermute | solution.py:279
  43.8 2.7 %prepare_up.1 = (bf16[512,512]{1,0:T(8,128)(2,1)S(1)}, bf16[512,512]{1,0:T(8,128)(2,1)S(1)}) custom-call(bf16[4,512,512]{2,1,0:T(8,128)(2,1)S(1)} %get-tuple-element.52.mh, bf16[4,512,512]{2,1,0:T(8,128)(2,1)S(1)} %get-tuple-element.53.ml), custom_call_target="tpu_custom_call" | custom-call | tf_op jit(solution)/shard_map/prepare_up/pallas_call | solution.py:57
  46.6 0.4 hop.12
  47.0 0.7 collective-permute-start.8
  47.7 0.4 hop.13
  48.1 0.7 collective-permute-start.9
  48.8 0.4 hop.14
  49.2 0.7 collective-permute-start.10
  50.3 0.7 collective-permute-start.11
  51.0 0.4 hop.16
  51.4 0.7 collective-permute-start.12
  52.5 0.7 collective-permute-start.13
  53.2 2.5 %turn.1 = (f32[4,32,512]{2,1,0:T(8,128)S(1)}, f32[32,512]{1,0:T(8,128)S(1)}) custom-call(f32[32,512]{1,0:T(8,128)S(1)} %get-tuple-element.69.held, f32[32,512]{1,0:T(8,128)S(1)} %collective-permute-done.13.came, f32[4,32,512]{2,1,0:T(8,128)S(1)} %get-tuple-element.71.cols, bf16[4,512,512]{2,1,0:T(8,128)(2,1)S(1)} %get-tuple-element.52.mh, ...), custom_call_target="tpu_custom_call" | custom-call | tf_op jit(solution)/shard_map/turn/pallas_call | solution.py:57
  55.7 0.7 collective-permute-start.14
  56.4 0.4 hop.18
  56.8 0.7 collective-permute-start.15
  57.5 0.4 hop.19
  57.9 0.7 collective-permute-start.16
  59.0 0.7 collective-permute-start.17
  60.1 0.7 collective-permute-start.18
  61.2 0.7 collective-permute-start.19
  62.3 1.3 collective-permute-start.20
  63.6 53.1 %collective-permute-done.20.came = f32[32,512]{1,0:T(8,128)S(1)} collective-permute-done((f32[32,512]{1,0:T(8,128)S(1)}, f32[32,512]{1,0:T(8,128)S(1)}, u32[]{:S(2)}, u32[]{:S(2)}) %collective-permute-start.20) | collective-permute-done | bytes 65568 | tf_op jit(solution)/shard_map/ppermute | solution.py:288
  116.7 1.5 rise.1
  118.2 1.6 %collective-permute-start.21 = (f32[2,32,512]{2,1,0:T(8,128)S(1)}, f32[2,32,512]{2,1,0:T(8,128)S(1)}, u32[]{:S(2)}, u32[]{:S(2)}) collective-permute-start(f32[2,32,512]{2,1,0:T(8,128)S(1)} %slice.22), channel_id=1, source_target_pairs={{0,4},{4,8},{8,12},{12,16},{16,20},{20,24},{24,28},{1,5},{5,9},{9,... | collective-permute-start | bytes 393224 | tf_op jit(solution)/shard_map/ppermute | solution.py:294
  119.8 1.3 collective-permute-start.22
  121.1 4.9 %collective-permute-done.22.ahead = f32[1,32,512]{2,1,0:T(8,128)S(1)} collective-permute-done((f32[1,32,512]{2,1,0:T(8,128)S(1)}, f32[1,32,512]{2,1,0:T(8,128)S(1)}, u32[]{:S(2)}, u32[]{:S(2)}) %collective-permute-start.22) | collective-permute-done | bytes 65568 | tf_op jit(solution)/shard_map/ppermute | solution.py:295
  126.0 1.0 pack.1
  127.0 3.5 %all-to-all-start.1 = ((f32[4,144,256]{2,1,0:T(8,128)}), f32[4,144,256]{2,1,0:T(8,128)S(1)}, u32[]{:S(2)}, u32[]{:S(2)}) async-start(f32[4,144,256]{2,1,0:T(8,128)} %pack.1), calls=%async_computation.1 | async-start | bytes 1179648 | tf_op jit(solution)/shard_map/all_to_all | solution.py:307
  130.5 9.4 %all-to-all-done.1.recv = f32[4,144,256]{2,1,0:T(8,128)S(1)} async-done(((f32[4,144,256]{2,1,0:T(8,128)}), f32[4,144,256]{2,1,0:T(8,128)S(1)}, u32[]{:S(2)}, u32[]{:S(2)}) %all-to-all-start.1) | async-done | bytes 589856 | tf_op jit(solution)/shard_map/all_to_all | solution.py:307
  139.9 1.7 %images.1 = (f32[4,128,128]{2,1,0:T(8,128)S(1)}, f32[4,128,128]{2,1,0:T(8,128)S(1)}, f32[4,128,128]{2,1,0:T(8,128)S(1)}, f32[32,128]{1,0:T(8,128)S(1)}) custom-call(s32[4]{0:T(128)S(1)} %pad_add_fusion.where, f32[4,144,256]{2,1,0:T(8,128)S(1)} %all-to-all-done.1.recv, f32[2,6,144,128]{3,2,1,0:T(8,128)S(1)} %pad_maximum_fusion.extended, ...), custom_call_target="tpu_custom_call" | custom-call | tf_op jit(solution)/shard_map/images/pallas_call | solution.py:57
  141.6 8.9 %all_to_all.21 = f32[32,1,128]{2,1,0:T(1,128)S(1)} all-to-all(f32[32,1,128]{2,1,0:T(1,128)S(1)} %bitcast.22), channel_id=1, replica_groups=mesh['layer'=8,'split'=4] {'layer','split'}, dimensions={0} | all-to-all | bytes 32768 | tf_op jit(solution)/shard_map/all_to_all | solution.py:317
  150.5 1.0 finish.1
  (39 shorter events, 3.3 us)
Async XLA Ops:
  0.6 17.7 %copy-start.1 = (f32[4,512,128]{2,1,0:T(8,128)S(1)}, f32[4,512,128]{2,1,0:T(8,128)}, u32[]{:S(2)}) copy-start(f32[4,512,128]{2,1,0:T(8,128)} %refs_0_.1) | copy-start | bytes 3145732
  0.6 14.3 %copy-start.2 = (f32[4,128,128]{2,1,0:T(8,128)S(1)}, f32[4,128,128]{2,1,0:T(8,128)}, u32[]{:S(2)}) copy-start(f32[4,128,128]{2,1,0:T(8,128)} %param.4) | copy-start | bytes 786436
  0.6 14.3 %copy-start = (f32[4,128,128]{2,1,0:T(8,128)S(1)}, f32[4,128,128]{2,1,0:T(8,128)}, u32[]{:S(2)}) copy-start(f32[4,128,128]{2,1,0:T(8,128)} %right_side.1) | copy-start | bytes 786436
  0.7 29.2 %collective-permute-start = (f32[4,512,128]{2,1,0:T(8,128)}, f32[4,512,128]{2,1,0:T(8,128)}, u32[]{:S(2)}, u32[]{:S(2)}) collective-permute-start(f32[4,512,128]{2,1,0:T(8,128)} %refs_0_.1), channel_id=1, source_target_pairs={{0,2},{1,3},{2,0},{3,1},{4,6},{5,7},{6,4},{7,5},{8,10},{9,11},{10,... | collective-permute-start | bytes 3145736 | tf_op jit(solution)/shard_map/ppermute | solution.py:253
  4.7 9.9 %collective-permute-start.1 = (f32[2,1,128,128]{3,2,1,0:T(8,128)S(1)}, f32[2,1,128,128]{3,2,1,0:T(8,128)S(1)}, u32[]{:S(2)}, u32[]{:S(2)}) collective-permute-start(f32[2,1,128,128]{3,2,1,0:T(8,128)S(1)} %get-tuple-element.98), channel_id=1, source_target_pairs={{0,4},{4,8},{8,12},{12,16},{16,20},{20,24},{24,28},{1,5},{5,9},{9,... | collective-permute-start | bytes 393224 | tf_op jit(solution)/shard_map/ppermute | solution.py:239
  8.1 6.9 %collective-permute-start.2 = (f32[2,1,128,128]{3,2,1,0:T(8,128)S(1)}, f32[2,1,128,128]{3,2,1,0:T(8,128)S(1)}, u32[]{:S(2)}, u32[]{:S(2)}) collective-permute-start(f32[2,1,128,128]{3,2,1,0:T(8,128)S(1)} %get-tuple-element.99), channel_id=1, source_target_pairs={{4,0},{8,4},{12,8},{16,12},{20,16},{24,20},{28,24},{5,1},{9,5},{13... | collective-permute-start | bytes 393224 | tf_op jit(solution)/shard_map/ppermute | solution.py:240
  11.2 18.7 %all-to-all-start = ((f32[4,4,32,128]{3,2,1,0:T(8,128)}), f32[4,4,32,128]{3,2,1,0:T(8,128)S(1)}, u32[]{:S(2)}, u32[]{:S(2)}) async-start(f32[4,4,32,128]{3,2,1,0:T(8,128)} %bitcast.17), calls=%async_computation | async-start | bytes 524288 | tf_op jit(solution)/shard_map/all_to_all | solution.py:233
  15.0 5.7 %collective-permute-start.3 = (f32[2,6,8,128]{3,2,1,0:T(8,128)S(1)}, f32[2,6,8,128]{3,2,1,0:T(8,128)S(1)}, u32[]{:S(2)}, u32[]{:S(2)}) collective-permute-start(f32[2,6,8,128]{3,2,1,0:T(8,128)S(1)} %get-tuple-element.96), channel_id=1, source_target_pairs={{0,1},{1,2},{2,3},{4,5},{5,6},{6,7},{8,9},{9,10},{10,11},{12,13},{... | collective-permute-start | bytes 147464 | tf_op jit(solution)/shard_map/ppermute | solution.py:243
  17.0 4.3 %collective-permute-start.4 = (f32[2,6,8,128]{3,2,1,0:T(8,128)S(1)}, f32[2,6,8,128]{3,2,1,0:T(8,128)S(1)}, u32[]{:S(2)}, u32[]{:S(2)}) collective-permute-start(f32[2,6,8,128]{3,2,1,0:T(8,128)S(1)} %get-tuple-element.97), channel_id=1, source_target_pairs={{1,0},{2,1},{3,2},{5,4},{6,5},{7,6},{9,8},{10,9},{11,10},{13,12},{... | collective-permute-start | bytes 147464 | tf_op jit(solution)/shard_map/ppermute | solution.py:244
  18.3 12.3 %collective-permute-start.5 = (f32[4,512,128]{2,1,0:T(8,128)S(1)}, f32[4,512,128]{2,1,0:T(8,128)}, u32[]{:S(2)}, u32[]{:S(2)}) collective-permute-start(f32[4,512,128]{2,1,0:T(8,128)S(1)} %copy-done.1), channel_id=1, source_target_pairs={{0,1},{1,0},{2,3},{3,2},{4,5},{5,4},{6,7},{7,6},{8,9},{9,8},{10,11... | collective-permute-start | bytes 3145736 | tf_op jit(solution)/shard_map/ppermute | solution.py:253
  29.9 3.3 %collective-permute-start.6 = (f32[4,512,128]{2,1,0:T(8,128)}, f32[4,512,128]{2,1,0:T(8,128)}, u32[]{:S(2)}, u32[]{:S(2)}) collective-permute-start(f32[4,512,128]{2,1,0:T(8,128)} %collective-permute-done.refs_1_), channel_id=1, source_target_pairs={{0,1},{1,0},{2,3},{3,2},{4,5},{5,4},{6,7},{7,6},{8,9},{9,8},{10,11... | collective-permute-start | bytes 3145736 | tf_op jit(solution)/shard_map/ppermute | solution.py:253
  40.2 6.3 %collective-permute-start.7 = (f32[32,512]{1,0:T(8,128)S(1)}, f32[32,512]{1,0:T(8,128)S(1)}, u32[]{:S(2)}, u32[]{:S(2)}) collective-permute-start(f32[32,512]{1,0:T(8,128)S(1)} %get-tuple-element.51.base), channel_id=1, source_target_pairs={{0,4},{1,5},{2,6},{3,7}} | collective-permute-start | bytes 196616 | tf_op jit(solution)/shard_map/ppermute | solution.py:279
  47.0 0.7 collective-permute-start.8
  48.1 0.7 collective-permute-start.9
  49.2 0.7 collective-permute-start.10
  50.3 0.7 collective-permute-start.11
  51.4 0.7 collective-permute-start.12
  52.5 0.7 collective-permute-start.13
  55.7 0.7 collective-permute-start.14
  56.8 0.7 collective-permute-start.15
  57.9 0.7 collective-permute-start.16
  59.0 0.7 collective-permute-start.17
  60.1 0.7 collective-permute-start.18
  61.2 0.7 collective-permute-start.19
  62.3 54.4 %collective-permute-start.20 = (f32[32,512]{1,0:T(8,128)S(1)}, f32[32,512]{1,0:T(8,128)S(1)}, u32[]{:S(2)}, u32[]{:S(2)}) collective-permute-start(f32[32,512]{1,0:T(8,128)S(1)} %get-tuple-element.86), channel_id=1, source_target_pairs={{4,0},{5,1},{6,2},{7,3}} | collective-permute-start | bytes 196616 | tf_op jit(solution)/shard_map/ppermute | solution.py:288
  118.2 7.8 %collective-permute-start.21 = (f32[2,32,512]{2,1,0:T(8,128)S(1)}, f32[2,32,512]{2,1,0:T(8,128)S(1)}, u32[]{:S(2)}, u32[]{:S(2)}) collective-permute-start(f32[2,32,512]{2,1,0:T(8,128)S(1)} %slice.22), channel_id=1, source_target_pairs={{0,4},{4,8},{8,12},{12,16},{16,20},{20,24},{24,28},{1,5},{5,9},{9,... | collective-permute-start | bytes 393224 | tf_op jit(solution)/shard_map/ppermute | solution.py:294
  119.8 6.2 %collective-permute-start.22 = (f32[1,32,512]{2,1,0:T(8,128)S(1)}, f32[1,32,512]{2,1,0:T(8,128)S(1)}, u32[]{:S(2)}, u32[]{:S(2)}) collective-permute-start(f32[1,32,512]{2,1,0:T(8,128)S(1)} %slice.23), channel_id=1, source_target_pairs={{4,0},{8,4},{12,8},{16,12},{20,16},{24,20},{28,24},{5,1},{9,5},{13... | collective-permute-start | bytes 196616 | tf_op jit(solution)/shard_map/ppermute | solution.py:295
  127.0 13.0 %all-to-all-start.1 = ((f32[4,144,256]{2,1,0:T(8,128)}), f32[4,144,256]{2,1,0:T(8,128)S(1)}, u32[]{:S(2)}, u32[]{:S(2)}) async-start(f32[4,144,256]{2,1,0:T(8,128)} %pack.1), calls=%async_computation.1 | async-start | bytes 1179648 | tf_op jit(solution)/shard_map/all_to_all | solution.py:307
